TPU v7x, 32 devices: a whole 2x2x4 slice. The times are simulated.
32 devices in a mesh: tm: 8 (over y, x, core), space: 4 (over z).
Axes of the slice: x: 2, y: 2, z: 4, core: 2. Of those that a mesh axis runs over, the one named last changes fastest.
Arguments:
- rhs: float32 [16, 1024, 1024], P('tm', 'space'), may hold values from -6 to 6
- guess: float32 [16, 1024, 1024], P('tm', 'space'), may hold values from -6 to 6
- diffusion: float32 [1024, 1024], P('space'), may hold values from 0.2 to 2
Outputs:
- solution: float32 [16, 1024, 1024], P('tm', 'space')
- norms: float32 [6], replicated
All inputs are finite; a program needn't handle non-finite values.
Results may differ from a plain program's by a relative error of at most 0.0001.
Values sent between devices are 32-bit elements; how exact they have to be, the bound alone decides.
A program may use at most 64 MiB of HBM per device.

v0:
```python
import jax
import jax.numpy as jnp
from jax import lax
from jax.sharding import PartitionSpec as P

LEVELS = 5


damping = 0.8


def with_halo(block, sides, width):
    for axis, dim in sides:
        count = lax.axis_size(axis)
        forward = [(i, i + 1) for i in range(count - 1)]
        backward = [(target, source) for source, target in forward]
        low = lax.ppermute(
            lax.slice_in_dim(block, block.shape[dim] - width, None, axis=dim), axis, forward
        )
        high = lax.ppermute(lax.slice_in_dim(block, 0, width, axis=dim), axis, backward)
        block = jnp.concatenate([low, block, high], axis=dim)
    return block


def shifted(value, axis, steps):
    count = lax.axis_size(axis)
    first, last = (max(0, -steps), min(count, count - steps))
    return lax.ppermute(value, axis, [(source, source + steps) for source in range(first, last)])


def from_partner(value, axis, apart):
    mask = 2**apart
    pairs = [(source, source ^ mask) for source in range(lax.axis_size(axis))]
    return lax.ppermute(value, axis, pairs)


def neighbours(field):
    rows = with_halo(field, (("space", 1),), 1)
    padded = jnp.pad(rows, ((0, 0), (0, 0), (1, 1)))
    total = padded[:, 2:, 1:-1] + padded[:, :-2, 1:-1]
    total = total + padded[:, 1:-1, 2:] + padded[:, 1:-1, :-2]
    return total


def residual(field, source, scaled, diag, stride):
    earlier = shifted(field[-1:], "tm", stride)
    before = jnp.concatenate([earlier, field[:-1]], axis=0)
    image = diag * field - scaled * neighbours(field) - before
    return source - image


def stride_of(level):
    if level == 0:
        return 1
    return 2 ** (level - 1)


def body(rhs, guess, diffusion):
    position = lax.axis_index("tm")
    cells = rhs.shape[1] * lax.axis_size("space") * rhs.shape[2]
    partials = []

    def weight_of(level):
        if level <= 1:
            return jnp.float32(1.0)
        stride = stride_of(level)
        return jnp.where(position % stride == stride - 1, 1.0, 0.0).astype(jnp.float32)

    def record(resid, level):
        local_part = jnp.sum(resid * resid) * weight_of(level)
        partials.append(local_part)

    sources = [rhs]
    fields = []
    field = guess
    for level in range(LEVELS - 1):
        source = sources[level]
        scaled = 2.0**level * diffusion
        diag = 1.0 + 4.0 * scaled
        stride = stride_of(level)
        if level == 0:
            field = field + damping * residual(field, source, scaled, diag, stride) / diag
        else:
            field = damping * source / diag
        resid = residual(field, source, scaled, diag, stride)
        record(resid, level)
        fields.append(field)
        if level == 0:
            coarse = resid[0:1] + resid[1:2]
        else:
            coarse = resid + from_partner(resid, "tm", level - 1)
        sources.append(coarse)
    level = LEVELS - 1
    source = sources[level]
    scaled = 2.0**level * diffusion
    diag = 1.0 + 4.0 * scaled
    stride = stride_of(level)
    field = damping * source / diag
    field = field + damping * residual(field, source, scaled, diag, stride) / diag
    resid = residual(field, source, scaled, diag, stride)
    record(resid, level)
    correction = field
    for level in range(LEVELS - 2, -1, -1):
        scaled = 2.0**level * diffusion
        diag = 1.0 + 4.0 * scaled
        stride = stride_of(level)
        field = fields[level] + correction
        field = field + damping * residual(field, sources[level], scaled, diag, stride) / diag
        correction = field
    scaled = 1.0 * diffusion
    diag = 1.0 + 4.0 * scaled
    resid = residual(correction, rhs, scaled, diag, 1)
    record(resid, 0)
    totals = lax.psum(jnp.stack(partials), ("tm", "space"))
    norms = jnp.sqrt(totals / cells)
    return (correction, norms)


def solution(mesh):
    in_specs = (P("tm", "space", None), P("tm", "space", None), P("space", None))
    out_specs = (P("tm", "space", None), P())
    return jax.shard_map(body, mesh=mesh, in_specs=in_specs, out_specs=out_specs, check_vma=False)
```

profile of v0, /device:TPU:0, one launch (start us, length us, event | category | flops | bytes accessed | tf_op | source)
XLA Modules:
  0.0 330.1 jit_solution(2631628433382767291)
XLA Ops:
  6.3 4.9 %collective-permute-start.1 = (f32[2,1,1024]{2,1,0:T(1,128)S(1)}, f32[2,1,1024]{2,1,0:T(1,128)S(1)}, u32[]{:S(2)}, u32[]{:S(2)}) collective-permute-start(f32[2,1,1024]{2,1,0:T(1,128)S(1)} %get-tuple-element.32), channel_id=1, source_target_pairs={{0,1},{1,2},{2,3},{4,5},{5,6},{6,7},{8,9},{9,10},{10,11},{12,13},{... | collective-permute-start | bytes 24584 | tf_op jit(solution)/shard_map/ppermute | solution.py:17
  15.5 7.8 %collective-permute-start.5 = (f32[1,256,1024]{2,1,0:T(8,128)S(1)}, f32[1,256,1024]{2,1,0:T(8,128)S(1)}, u32[]{:S(2)}, u32[]{:S(2)}) collective-permute-start(f32[1,256,1024]{2,1,0:T(8,128)S(1)} %get-tuple-element.28), channel_id=1, source_target_pairs={{0,4},{4,8},{8,12},{12,16},{16,20},{20,24},{24,28},{1,5},{5,9},{9,... | collective-permute-start | bytes 3145736 | tf_op jit(solution)/shard_map/ppermute | solution.py:28
  24.6 4.5 %collective-permute-start.4 = (f32[2,1,1024]{2,1,0:T(1,128)S(1)}, f32[2,1,1024]{2,1,0:T(1,128)S(1)}, u32[]{:S(2)}, u32[]{:S(2)}) collective-permute-start(f32[2,1,1024]{2,1,0:T(1,128)S(1)} %get-tuple-element.26), channel_id=1, source_target_pairs={{0,1},{1,2},{2,3},{4,5},{5,6},{6,7},{8,9},{9,10},{10,11},{12,13},{... | collective-permute-start | bytes 24584 | tf_op jit(solution)/shard_map/ppermute | solution.py:17
  34.0 8.1 %collective-permute-start.8 = (f32[1,256,1024]{2,1,0:T(8,128)S(1)}, f32[1,256,1024]{2,1,0:T(8,128)S(1)}, u32[]{:S(2)}, u32[]{:S(2)}) collective-permute-start(f32[1,256,1024]{2,1,0:T(8,128)S(1)} %bitcast_divide_fusion.3), channel_id=1, source_target_pairs={{0,4},{4,8},{8,12},{12,16},{16,20},{20,24},{24,28},{1,5},{5,9},{9,... | collective-permute-start | bytes 3145736 | tf_op jit(solution)/shard_map/ppermute | solution.py:28
  43.4 4.5 %collective-permute-start.7 = (f32[1,1,1024]{2,1,0:T(1,128)S(1)}, f32[1,1,1024]{2,1,0:T(1,128)S(1)}, u32[]{:S(2)}, u32[]{:S(2)}) collective-permute-start(f32[1,1,1024]{2,1,0:T(1,128)S(1)} %get-tuple-element.48), channel_id=1, source_target_pairs={{0,1},{1,2},{2,3},{4,5},{5,6},{6,7},{8,9},{9,10},{10,11},{12,13},{... | collective-permute-start | bytes 12296 | tf_op jit(solution)/shard_map/ppermute | solution.py:17
  51.2 6.5 %collective-permute-start.9 = (f32[1,256,1024]{2,1,0:T(8,128)S(1)}, f32[1,256,1024]{2,1,0:T(8,128)S(1)}, u32[]{:S(2)}, u32[]{:S(2)}) collective-permute-start(f32[1,256,1024]{2,1,0:T(8,128)S(1)} %get-tuple-element.7), channel_id=1, source_target_pairs={{0,4},{4,0},{8,12},{12,8},{16,20},{20,16},{24,28},{28,24},{1,5},{5... | collective-permute-start | bytes 3145736 | tf_op jit(solution)/shard_map/ppermute | solution.py:34
  60.4 5.3 %collective-permute-start.12 = (f32[1,256,1024]{2,1,0:T(8,128)S(1)}, f32[1,256,1024]{2,1,0:T(8,128)S(1)}, u32[]{:S(2)}, u32[]{:S(2)}) collective-permute-start(f32[1,256,1024]{2,1,0:T(8,128)S(1)} %get-tuple-element.16), channel_id=1, source_target_pairs={{0,8},{4,12},{8,16},{12,20},{16,24},{20,28},{1,9},{5,13},{9,17},{1... | collective-permute-start | bytes 3145736 | tf_op jit(solution)/shard_map/ppermute | solution.py:28
  67.0 4.5 %collective-permute-start.11 = (f32[1,1,1024]{2,1,0:T(1,128)S(1)}, f32[1,1,1024]{2,1,0:T(1,128)S(1)}, u32[]{:S(2)}, u32[]{:S(2)}) collective-permute-start(f32[1,1,1024]{2,1,0:T(1,128)S(1)} %get-tuple-element.46), channel_id=1, source_target_pairs={{0,1},{1,2},{2,3},{4,5},{5,6},{6,7},{8,9},{9,10},{10,11},{12,13},{... | collective-permute-start | bytes 12296 | tf_op jit(solution)/shard_map/ppermute | solution.py:17
  73.2 15.3 %collective-permute-done.12 = f32[1,256,1024]{2,1,0:T(8,128)S(1)} collective-permute-done((f32[1,256,1024]{2,1,0:T(8,128)S(1)}, f32[1,256,1024]{2,1,0:T(8,128)S(1)}, u32[]{:S(2)}, u32[]{:S(2)}) %collective-permute-start.12) | collective-permute-done | bytes 1048608 | tf_op jit(solution)/shard_map/ppermute | solution.py:28
  93.4 22.6 %collective-permute-done.13 = f32[1,256,1024]{2,1,0:T(8,128)S(1)} collective-permute-done((f32[1,256,1024]{2,1,0:T(8,128)S(1)}, f32[1,256,1024]{2,1,0:T(8,128)S(1)}, u32[]{:S(2)}, u32[]{:S(2)}) %collective-permute-start.13) | collective-permute-done | bytes 1048608 | tf_op jit(solution)/shard_map/ppermute | solution.py:34
  116.4 5.6 %collective-permute-start.16 = (f32[1,256,1024]{2,1,0:T(8,128)S(1)}, f32[1,256,1024]{2,1,0:T(8,128)S(1)}, u32[]{:S(2)}, u32[]{:S(2)}) collective-permute-start(f32[1,256,1024]{2,1,0:T(8,128)S(1)} %get-tuple-element.14), channel_id=1, source_target_pairs={{0,16},{4,20},{8,24},{12,28},{1,17},{5,21},{9,25},{13,29},{2,18},{... | collective-permute-start | bytes 3145736 | tf_op jit(solution)/shard_map/ppermute | solution.py:28
  123.4 4.5 %collective-permute-start.15 = (f32[1,1,1024]{2,1,0:T(1,128)S(1)}, f32[1,1,1024]{2,1,0:T(1,128)S(1)}, u32[]{:S(2)}, u32[]{:S(2)}) collective-permute-start(f32[1,1,1024]{2,1,0:T(1,128)S(1)} %get-tuple-element.44), channel_id=1, source_target_pairs={{0,1},{1,2},{2,3},{4,5},{5,6},{6,7},{8,9},{9,10},{10,11},{12,13},{... | collective-permute-start | bytes 12296 | tf_op jit(solution)/shard_map/ppermute | solution.py:17
  129.7 13.3 %collective-permute-done.16 = f32[1,256,1024]{2,1,0:T(8,128)S(1)} collective-permute-done((f32[1,256,1024]{2,1,0:T(8,128)S(1)}, f32[1,256,1024]{2,1,0:T(8,128)S(1)}, u32[]{:S(2)}, u32[]{:S(2)}) %collective-permute-start.16) | collective-permute-done | bytes 1048608 | tf_op jit(solution)/shard_map/ppermute | solution.py:28
  146.9 20.9 %collective-permute-done.17 = f32[1,256,1024]{2,1,0:T(8,128)S(1)} collective-permute-done((f32[1,256,1024]{2,1,0:T(8,128)S(1)}, f32[1,256,1024]{2,1,0:T(8,128)S(1)}, u32[]{:S(2)}, u32[]{:S(2)}) %collective-permute-start.17) | collective-permute-done | bytes 1048608 | tf_op jit(solution)/shard_map/ppermute | solution.py:34
  170.2 4.7 %collective-permute-start.19 = (f32[1,1,1024]{2,1,0:T(1,128)S(1)}, f32[1,1,1024]{2,1,0:T(1,128)S(1)}, u32[]{:S(2)}, u32[]{:S(2)}) collective-permute-start(f32[1,1,1024]{2,1,0:T(1,128)S(1)} %get-tuple-element.42), channel_id=1, source_target_pairs={{0,1},{1,2},{2,3},{4,5},{5,6},{6,7},{8,9},{9,10},{10,11},{12,13},{... | collective-permute-start | bytes 12296 | tf_op jit(solution)/shard_map/ppermute | solution.py:17
  183.5 4.8 %collective-permute-start.22 = (f32[1,1,1024]{2,1,0:T(1,128)S(1)}, f32[1,1,1024]{2,1,0:T(1,128)S(1)}, u32[]{:S(2)}, u32[]{:S(2)}) collective-permute-start(f32[1,1,1024]{2,1,0:T(1,128)S(1)} %get-tuple-element.40), channel_id=1, source_target_pairs={{0,1},{1,2},{2,3},{4,5},{5,6},{6,7},{8,9},{9,10},{10,11},{12,13},{... | collective-permute-start | bytes 12296 | tf_op jit(solution)/shard_map/ppermute | solution.py:17
  190.0 10.2 %collective-permute-done.23 = f32[1,256,1024]{2,1,0:T(8,128)S(1)} collective-permute-done((f32[1,256,1024]{2,1,0:T(8,128)S(1)}, f32[1,256,1024]{2,1,0:T(8,128)S(1)}, u32[]{:S(2)}, u32[]{:S(2)}) %collective-permute-start.23) | collective-permute-done | bytes 1048608 | tf_op jit(solution)/shard_map/ppermute | solution.py:28
  205.8 4.5 %collective-permute-start.25 = (f32[1,1,1024]{2,1,0:T(1,128)S(1)}, f32[1,1,1024]{2,1,0:T(1,128)S(1)}, u32[]{:S(2)}, u32[]{:S(2)}) collective-permute-start(f32[1,1,1024]{2,1,0:T(1,128)S(1)} %get-tuple-element.38), channel_id=1, source_target_pairs={{0,1},{1,2},{2,3},{4,5},{5,6},{6,7},{8,9},{9,10},{10,11},{12,13},{... | collective-permute-start | bytes 12296 | tf_op jit(solution)/shard_map/ppermute | solution.py:17
  212.1 9.9 %collective-permute-done.26 = f32[1,256,1024]{2,1,0:T(8,128)S(1)} collective-permute-done((f32[1,256,1024]{2,1,0:T(8,128)S(1)}, f32[1,256,1024]{2,1,0:T(8,128)S(1)}, u32[]{:S(2)}, u32[]{:S(2)}) %collective-permute-start.26) | collective-permute-done | bytes 1048608 | tf_op jit(solution)/shard_map/ppermute | solution.py:28
  234.7 10.2 %collective-permute-start.32 = (f32[1,256,1024]{2,1,0:T(8,128)}, f32[1,256,1024]{2,1,0:T(8,128)}, u32[]{:S(2)}, u32[]{:S(2)}) collective-permute-start(f32[1,256,1024]{2,1,0:T(8,128)} %get-tuple-element.22), channel_id=1, source_target_pairs={{0,4},{4,8},{8,12},{12,16},{16,20},{20,24},{24,28},{1,5},{5,9},{9,... | collective-permute-start | bytes 3145736 | tf_op jit(solution)/shard_map/ppermute | solution.py:28
  247.4 4.5 %collective-permute-start.31 = (f32[2,1,1024]{2,1,0:T(1,128)S(1)}, f32[2,1,1024]{2,1,0:T(1,128)S(1)}, u32[]{:S(2)}, u32[]{:S(2)}) collective-permute-start(f32[2,1,1024]{2,1,0:T(1,128)S(1)} %get-tuple-element.24), channel_id=1, source_target_pairs={{0,1},{1,2},{2,3},{4,5},{5,6},{6,7},{8,9},{9,10},{10,11},{12,13},{... | collective-permute-start | bytes 24584 | tf_op jit(solution)/shard_map/ppermute | solution.py:17
  254.8 4.8 %collective-permute-start.34 = (f32[1,1,1024]{2,1,0:T(1,128)S(1)}, f32[1,1,1024]{2,1,0:T(1,128)S(1)}, u32[]{:S(2)}, u32[]{:S(2)}) collective-permute-start(f32[1,1,1024]{2,1,0:T(1,128)S(1)} %get-tuple-element.34), channel_id=1, source_target_pairs={{0,1},{1,2},{2,3},{4,5},{5,6},{6,7},{8,9},{9,10},{10,11},{12,13},{... | collective-permute-start | bytes 12296 | tf_op jit(solution)/shard_map/ppermute | solution.py:17
  270.1 4.9 %collective-permute-start.37 = (f32[2,1,1024]{2,1,0:T(1,128)S(1)}, f32[2,1,1024]{2,1,0:T(1,128)S(1)}, u32[]{:S(2)}, u32[]{:S(2)}) collective-permute-start(f32[2,1,1024]{2,1,0:T(1,128)S(1)} %get-tuple-element.20), channel_id=1, source_target_pairs={{0,1},{1,2},{2,3},{4,5},{5,6},{6,7},{8,9},{9,10},{10,11},{12,13},{... | collective-permute-start | bytes 24584 | tf_op jit(solution)/shard_map/ppermute | solution.py:17
  284.7 44.9 %psum.7 = f32[6]{0:T(128)S(1)} all-reduce(f32[6]{0:T(128)S(1)} %stack.27), channel_id=1, replica_groups=mesh['tm'=8,'space'=4] {'tm','space'}, use_global_device_ids=true, to_apply=%region_6.7 | all-reduce | flops 6 | bytes 48 | tf_op jit(solution)/shard_map/psum | solution.py:114
  (133 shorter events, 94.8 us)
Async XLA Ops:
  2.5 10.9 %collective-permute-start.2 = (f32[1,256,1024]{2,1,0:T(8,128)S(1)}, f32[1,256,1024]{2,1,0:T(8,128)S(1)}, u32[]{:S(2)}, u32[]{:S(2)}) collective-permute-start(f32[1,256,1024]{2,1,0:T(8,128)S(1)} %get-tuple-element.30), channel_id=1, source_target_pairs={{0,4},{4,8},{8,12},{12,16},{16,20},{20,24},{24,28},{1,5},{5,9},{9,... | collective-permute-start | bytes 3145736 | tf_op jit(solution)/shard_map/ppermute | solution.py:28
  5.0 6.4 %collective-permute-start = (f32[2,1,1024]{2,1,0:T(1,128)S(1)}, f32[2,1,1024]{2,1,0:T(1,128)S(1)}, u32[]{:S(2)}, u32[]{:S(2)}) collective-permute-start(f32[2,1,1024]{2,1,0:T(1,128)S(1)} %get-tuple-element.33), channel_id=1, source_target_pairs={{1,0},{2,1},{3,2},{5,4},{6,5},{7,6},{9,8},{10,9},{11,10},{13,12},{... | collective-permute-start | bytes 24584 | tf_op jit(solution)/shard_map/ppermute | solution.py:20
  6.3 6.3 %collective-permute-start.1 = (f32[2,1,1024]{2,1,0:T(1,128)S(1)}, f32[2,1,1024]{2,1,0:T(1,128)S(1)}, u32[]{:S(2)}, u32[]{:S(2)}) collective-permute-start(f32[2,1,1024]{2,1,0:T(1,128)S(1)} %get-tuple-element.32), channel_id=1, source_target_pairs={{0,1},{1,2},{2,3},{4,5},{5,6},{6,7},{8,9},{9,10},{10,11},{12,13},{... | collective-permute-start | bytes 24584 | tf_op jit(solution)/shard_map/ppermute | solution.py:17
  15.5 15.8 %collective-permute-start.5 = (f32[1,256,1024]{2,1,0:T(8,128)S(1)}, f32[1,256,1024]{2,1,0:T(8,128)S(1)}, u32[]{:S(2)}, u32[]{:S(2)}) collective-permute-start(f32[1,256,1024]{2,1,0:T(8,128)S(1)} %get-tuple-element.28), channel_id=1, source_target_pairs={{0,4},{4,8},{8,12},{12,16},{16,20},{20,24},{24,28},{1,5},{5,9},{9,... | collective-permute-start | bytes 3145736 | tf_op jit(solution)/shard_map/ppermute | solution.py:28
  34.0 15.7 %collective-permute-start.8 = (f32[1,256,1024]{2,1,0:T(8,128)S(1)}, f32[1,256,1024]{2,1,0:T(8,128)S(1)}, u32[]{:S(2)}, u32[]{:S(2)}) collective-permute-start(f32[1,256,1024]{2,1,0:T(8,128)S(1)} %bitcast_divide_fusion.3), channel_id=1, source_target_pairs={{0,4},{4,8},{8,12},{12,16},{16,20},{20,24},{24,28},{1,5},{5,9},{9,... | collective-permute-start | bytes 3145736 | tf_op jit(solution)/shard_map/ppermute | solution.py:28
  51.2 8.8 %collective-permute-start.9 = (f32[1,256,1024]{2,1,0:T(8,128)S(1)}, f32[1,256,1024]{2,1,0:T(8,128)S(1)}, u32[]{:S(2)}, u32[]{:S(2)}) collective-permute-start(f32[1,256,1024]{2,1,0:T(8,128)S(1)} %get-tuple-element.7), channel_id=1, source_target_pairs={{0,4},{4,0},{8,12},{12,8},{16,20},{20,16},{24,28},{28,24},{1,5},{5... | collective-permute-start | bytes 3145736 | tf_op jit(solution)/shard_map/ppermute | solution.py:34
  60.4 28.1 %collective-permute-start.12 = (f32[1,256,1024]{2,1,0:T(8,128)S(1)}, f32[1,256,1024]{2,1,0:T(8,128)S(1)}, u32[]{:S(2)}, u32[]{:S(2)}) collective-permute-start(f32[1,256,1024]{2,1,0:T(8,128)S(1)} %get-tuple-element.16), channel_id=1, source_target_pairs={{0,8},{4,12},{8,16},{12,20},{16,24},{20,28},{1,9},{5,13},{9,17},{1... | collective-permute-start | bytes 3145736 | tf_op jit(solution)/shard_map/ppermute | solution.py:28
  90.0 26.0 %collective-permute-start.13 = (f32[1,256,1024]{2,1,0:T(8,128)S(1)}, f32[1,256,1024]{2,1,0:T(8,128)S(1)}, u32[]{:S(2)}, u32[]{:S(2)}) collective-permute-start(f32[1,256,1024]{2,1,0:T(8,128)S(1)} %get-tuple-element.5), channel_id=1, source_target_pairs={{0,8},{4,12},{8,0},{12,4},{16,24},{20,28},{24,16},{28,20},{1,9},{5... | collective-permute-start | bytes 3145736 | tf_op jit(solution)/shard_map/ppermute | solution.py:34
  116.4 26.6 %collective-permute-start.16 = (f32[1,256,1024]{2,1,0:T(8,128)S(1)}, f32[1,256,1024]{2,1,0:T(8,128)S(1)}, u32[]{:S(2)}, u32[]{:S(2)}) collective-permute-start(f32[1,256,1024]{2,1,0:T(8,128)S(1)} %get-tuple-element.14), channel_id=1, source_target_pairs={{0,16},{4,20},{8,24},{12,28},{1,17},{5,21},{9,25},{13,29},{2,18},{... | collective-permute-start | bytes 3145736 | tf_op jit(solution)/shard_map/ppermute | solution.py:28
  144.4 23.4 %collective-permute-start.17 = (f32[1,256,1024]{2,1,0:T(8,128)S(1)}, f32[1,256,1024]{2,1,0:T(8,128)S(1)}, u32[]{:S(2)}, u32[]{:S(2)}) collective-permute-start(f32[1,256,1024]{2,1,0:T(8,128)S(1)} %get-tuple-element.3), channel_id=1, source_target_pairs={{0,16},{4,20},{8,24},{12,28},{16,0},{20,4},{24,8},{28,12},{1,17},{... | collective-permute-start | bytes 3145736 | tf_op jit(solution)/shard_map/ppermute | solution.py:34
  168.2 8.3 %collective-permute-start.20 = (f32[1,256,1024]{2,1,0:T(8,128)S(1)}, f32[1,256,1024]{2,1,0:T(8,128)S(1)}, u32[]{:S(2)}, u32[]{:S(2)}) collective-permute-start(f32[1,256,1024]{2,1,0:T(8,128)S(1)} %get-tuple-element.12), channel_id=1, source_target_pairs={} | collective-permute-start | bytes 3145736 | tf_op jit(solution)/shard_map/ppermute | solution.py:28
  178.5 21.8 %collective-permute-start.23 = (f32[1,256,1024]{2,1,0:T(8,128)S(1)}, f32[1,256,1024]{2,1,0:T(8,128)S(1)}, u32[]{:S(2)}, u32[]{:S(2)}) collective-permute-start(f32[1,256,1024]{2,1,0:T(8,128)S(1)} %get-tuple-element.10), channel_id=1, source_target_pairs={{0,16},{4,20},{8,24},{12,28},{1,17},{5,21},{9,25},{13,29},{2,18},{... | collective-permute-start | bytes 3145736 | tf_op jit(solution)/shard_map/ppermute | solution.py:28
  183.5 6.1 %collective-permute-start.22 = (f32[1,1,1024]{2,1,0:T(1,128)S(1)}, f32[1,1,1024]{2,1,0:T(1,128)S(1)}, u32[]{:S(2)}, u32[]{:S(2)}) collective-permute-start(f32[1,1,1024]{2,1,0:T(1,128)S(1)} %get-tuple-element.40), channel_id=1, source_target_pairs={{0,1},{1,2},{2,3},{4,5},{5,6},{6,7},{8,9},{9,10},{10,11},{12,13},{... | collective-permute-start | bytes 12296 | tf_op jit(solution)/shard_map/ppermute | solution.py:17
  201.4 20.6 %collective-permute-start.26 = (f32[1,256,1024]{2,1,0:T(8,128)S(1)}, f32[1,256,1024]{2,1,0:T(8,128)S(1)}, u32[]{:S(2)}, u32[]{:S(2)}) collective-permute-start(f32[1,256,1024]{2,1,0:T(8,128)S(1)} %fusion.61), channel_id=1, source_target_pairs={{0,8},{4,12},{8,16},{12,20},{16,24},{20,28},{1,9},{5,13},{9,17},{1... | collective-permute-start | bytes 3145736 | tf_op jit(solution)/shard_map/ppermute | solution.py:28
  223.0 9.0 %collective-permute-start.29 = (f32[1,256,1024]{2,1,0:T(8,128)S(1)}, f32[1,256,1024]{2,1,0:T(8,128)S(1)}, u32[]{:S(2)}, u32[]{:S(2)}) collective-permute-start(f32[1,256,1024]{2,1,0:T(8,128)S(1)} %fusion.52), channel_id=1, source_target_pairs={{0,4},{4,8},{8,12},{12,16},{16,20},{20,24},{24,28},{1,5},{5,9},{9,... | collective-permute-start | bytes 3145736 | tf_op jit(solution)/shard_map/ppermute | solution.py:28
  234.7 25.8 %collective-permute-start.32 = (f32[1,256,1024]{2,1,0:T(8,128)}, f32[1,256,1024]{2,1,0:T(8,128)}, u32[]{:S(2)}, u32[]{:S(2)}) collective-permute-start(f32[1,256,1024]{2,1,0:T(8,128)} %get-tuple-element.22), channel_id=1, source_target_pairs={{0,4},{4,8},{8,12},{12,16},{16,20},{20,24},{24,28},{1,5},{5,9},{9,... | collective-permute-start | bytes 3145736 | tf_op jit(solution)/shard_map/ppermute | solution.py:28
  246.1 8.7 %collective-permute-start.30 = (f32[2,1,1024]{2,1,0:T(1,128)S(1)}, f32[2,1,1024]{2,1,0:T(1,128)S(1)}, u32[]{:S(2)}, u32[]{:S(2)}) collective-permute-start(f32[2,1,1024]{2,1,0:T(1,128)S(1)} %get-tuple-element.25), channel_id=1, source_target_pairs={{1,0},{2,1},{3,2},{5,4},{6,5},{7,6},{9,8},{10,9},{11,10},{13,12},{... | collective-permute-start | bytes 24584 | tf_op jit(solution)/shard_map/ppermute | solution.py:20
  247.4 12.2 %collective-permute-start.31 = (f32[2,1,1024]{2,1,0:T(1,128)S(1)}, f32[2,1,1024]{2,1,0:T(1,128)S(1)}, u32[]{:S(2)}, u32[]{:S(2)}) collective-permute-start(f32[2,1,1024]{2,1,0:T(1,128)S(1)} %get-tuple-element.24), channel_id=1, source_target_pairs={{0,1},{1,2},{2,3},{4,5},{5,6},{6,7},{8,9},{9,10},{10,11},{12,13},{... | collective-permute-start | bytes 24584 | tf_op jit(solution)/shard_map/ppermute | solution.py:17
  252.7 22.3 %collective-permute-start.35 = (f32[1,256,1024]{2,1,0:T(8,128)}, f32[1,256,1024]{2,1,0:T(8,128)S(1)}, u32[]{:S(2)}, u32[]{:S(2)}) collective-permute-start(f32[1,256,1024]{2,1,0:T(8,128)} %get-tuple-element.11), channel_id=1, source_target_pairs={} | collective-permute-start | bytes 3145736 | tf_op jit(solution)/shard_map/ppermute | solution.py:28
  253.5 14.9 %collective-permute-start.33 = (f32[1,1,1024]{2,1,0:T(1,128)S(1)}, f32[1,1,1024]{2,1,0:T(1,128)S(1)}, u32[]{:S(2)}, u32[]{:S(2)}) collective-permute-start(f32[1,1,1024]{2,1,0:T(1,128)S(1)} %get-tuple-element.35), channel_id=1, source_target_pairs={{1,0},{2,1},{3,2},{5,4},{6,5},{7,6},{9,8},{10,9},{11,10},{13,12},{... | collective-permute-start | bytes 12296 | tf_op jit(solution)/shard_map/ppermute | solution.py:20
  254.8 13.6 %collective-permute-start.34 = (f32[1,1,1024]{2,1,0:T(1,128)S(1)}, f32[1,1,1024]{2,1,0:T(1,128)S(1)}, u32[]{:S(2)}, u32[]{:S(2)}) collective-permute-start(f32[1,1,1024]{2,1,0:T(1,128)S(1)} %get-tuple-element.34), channel_id=1, source_target_pairs={{0,1},{1,2},{2,3},{4,5},{5,6},{6,7},{8,9},{9,10},{10,11},{12,13},{... | collective-permute-start | bytes 12296 | tf_op jit(solution)/shard_map/ppermute | solution.py:17
  265.0 13.1 %collective-permute-start.38 = (f32[1,256,1024]{2,1,0:T(8,128)}, f32[1,256,1024]{2,1,0:T(8,128)}, u32[]{:S(2)}, u32[]{:S(2)}) collective-permute-start(f32[1,256,1024]{2,1,0:T(8,128)} %get-tuple-element.18), channel_id=1, source_target_pairs={{0,4},{4,8},{8,12},{12,16},{16,20},{20,24},{24,28},{1,5},{5,9},{9,... | collective-permute-start | bytes 3145736 | tf_op jit(solution)/shard_map/ppermute | solution.py:28
  268.8 8.4 %collective-permute-start.36 = (f32[2,1,1024]{2,1,0:T(1,128)S(1)}, f32[2,1,1024]{2,1,0:T(1,128)S(1)}, u32[]{:S(2)}, u32[]{:S(2)}) collective-permute-start(f32[2,1,1024]{2,1,0:T(1,128)S(1)} %get-tuple-element.21), channel_id=1, source_target_pairs={{1,0},{2,1},{3,2},{5,4},{6,5},{7,6},{9,8},{10,9},{11,10},{13,12},{... | collective-permute-start | bytes 24584 | tf_op jit(solution)/shard_map/ppermute | solution.py:20
  270.1 7.1 %collective-permute-start.37 = (f32[2,1,1024]{2,1,0:T(1,128)S(1)}, f32[2,1,1024]{2,1,0:T(1,128)S(1)}, u32[]{:S(2)}, u32[]{:S(2)}) collective-permute-start(f32[2,1,1024]{2,1,0:T(1,128)S(1)} %get-tuple-element.20), channel_id=1, source_target_pairs={{0,1},{1,2},{2,3},{4,5},{5,6},{6,7},{8,9},{9,10},{10,11},{12,13},{... | collective-permute-start | bytes 24584 | tf_op jit(solution)/shard_map/ppermute | solution.py:17
  (30 other events, 185.9 us)
where the time goes:
time: 331 us; the launch traced here: 330 us
  starting transfers between devices  136 us (41%)
  waiting for transfers between devices  106 us (32%)
  blocking collectives  44.9 us (14%)
  other arithmetic  30.2 us (9%)
  local copies, waits for them, and re-layouts  9.38 us (3%)
  between operations  3.35 us (1%)
    ppermute x12, starting transfers between devices, with_halo(): lax.ppermute(lax.slice_in_dim(block, block.shape[dim] - width, None, axis...  56 us
    ppermute x12, starting transfers between devices, shifted(): lax.ppermute(value, axis, [(source, source + steps) for source in range(f...  52.4 us
    ppermute x12, waiting for transfers between devices, shifted(): lax.ppermute(value, axis, [(source, source + steps) for source in range(f...  48.7 us
    ppermute x3, waiting for transfers between devices, from_partner(): return lax.ppermute(value, axis, pairs)  45.8 us
    psum x1, blocking collectives, body(): totals = lax.psum(jnp.stack(partials), ('tm', 'space'))  44.9 us
    ppermute x12, starting transfers between devices, with_halo(): lax.ppermute(lax.slice_in_dim(block, 0, width, axis=dim), axis, backward)  15.5 us
    ppermute x3, starting transfers between devices, from_partner(): return lax.ppermute(value, axis, pairs)  12.4 us
    reduce_sum x6, other arithmetic, record(): local_part = jnp.sum(resid * resid) * weight_of(level)  11.6 us
  transfers between devices with their start and end apart: 39, of which 16 were waited for; matrix products, arithmetic and copies ran while one was open for 4% of the time, Pallas kernels for 0%

commit v1 on v0

--- a/solution.py
+++ b/solution.py
@@ -1,6 +1,10 @@
+import functools
+
 import jax
 import jax.numpy as jnp
 from jax import lax
+from jax.experimental import pallas as pl
+from jax.experimental.pallas import tpu as pltpu
 from jax.sharding import PartitionSpec as P
 
 LEVELS = 5
@@ -116,7 +120,620 @@
     return (correction, norms)
 
 
+DEVICE = pl.DeviceIdType.MESH
+TILE = 8
+EDGE = 2 * TILE
+
+
+def cycle_kernel(
+    strips, devices, cells,
+    rhs_in, guess_in, diff_in, out, norms_out,
+    rhs, guess, diff, v0, g1, v1, r1, v1f, sol, guess_e, v0_e, v1_e, v1f_e, sol_e,
+    pair, g2h, v2, c_g2, c_v2, c_g3, c_v3, c_g4, c_v4, c_v4b, acc, tile, gathered, gathered_z,
+    load_sem, store_sem, zs_sem, zr_sem, ts_sem, tr_sem, ps_sem, pr_sem, as_sem, ar_sem, al_sem,
+    bs_sem, br_sem, bl_sem, ns_sem, nr_sem, ms_sem, mr_sem,
+):
+    me = lax.axis_index("tm")
+    strip = lax.axis_index("space")
+    rows, width = rhs_in.shape[1], rhs_in.shape[2]
+    chips = devices // 2
+    core = lax.rem(me, 2)
+    chip = me // 2
+    low, high = EDGE, EDGE + rows
+    first, last = me == 0, me == devices - 1
+    top, bottom = strip == 0, strip == strips - 1
+    piece = rows // devices
+
+    def aligned(value):
+        return pl.multiple_of(value, TILE)
+
+    def tm_copy(src, dst, send, recv, target):
+        return pltpu.make_async_remote_copy(
+            src_ref=src, dst_ref=dst, send_sem=send, recv_sem=recv,
+            device_id={"tm": target, "space": strip}, device_id_type=DEVICE,
+        )
+
+    def space_copy(src, dst, send, recv, target):
+        return pltpu.make_async_remote_copy(
+            src_ref=src, dst_ref=dst, send_sem=send, recv_sem=recv,
+            device_id={"tm": me, "space": target}, device_id_type=DEVICE,
+        )
+
+    later = jnp.minimum(me + 1, devices - 1)
+    loads = [
+        pltpu.make_async_copy(guess_in, guess.at[:, low:high], load_sem.at[0]),
+        pltpu.make_async_copy(diff_in, diff.at[low:high], load_sem.at[1]),
+        pltpu.make_async_copy(rhs_in, rhs.at[:, low:high], load_sem.at[2]),
+    ]
+    for copy in loads:
+        copy.start()
+
+    barrier = pltpu.get_barrier_semaphore()
+    for i in range(1, devices):
+        pl.semaphore_signal(
+            barrier, inc=1, device_id={"tm": lax.rem(me + i, devices), "space": strip}, device_id_type=DEVICE
+        )
+    for i in range(1, strips):
+        pl.semaphore_signal(
+            barrier, inc=1, device_id={"tm": me, "space": lax.rem(strip + i, strips)}, device_id_type=DEVICE
+        )
+    pl.semaphore_wait(barrier, devices + strips - 2)
+
+    down = jnp.minimum(strip + 1, strips - 1)
+    up = jnp.maximum(strip - 1, 0)
+
+    def halo_pair(index, tail, head, low_dst, high_dst):
+        return (
+            space_copy(tail, low_dst, zs_sem.at[index, 0], zr_sem.at[index, 0], down),
+            space_copy(head, high_dst, zs_sem.at[index, 1], zr_sem.at[index, 1], up),
+        )
+
+    before_low, after_high = slice(low - TILE, low), slice(high, high + TILE)
+    halos = [
+        halo_pair(
+            0, guess_in.at[:, rows - TILE:rows], guess_in.at[:, 0:TILE],
+            guess.at[:, before_low], guess.at[:, after_high],
+        ),
+        halo_pair(
+            1, diff_in.at[rows - TILE:rows], diff_in.at[0:TILE], diff.at[before_low], diff.at[after_high],
+        ),
+        halo_pair(
+            2, rhs_in.at[:, rows - TILE:rows], rhs_in.at[:, 0:TILE],
+            rhs.at[:, before_low], rhs.at[:, after_high],
+        ),
+    ]
+
+    def start_halo(pair_of):
+        @pl.when(jnp.logical_not(bottom))
+        def _():
+            pair_of[0].start()
+
+        @pl.when(jnp.logical_not(top))
+        def _():
+            pair_of[1].start()
+
+    def finish_halo(pair_of):
+        @pl.when(jnp.logical_not(top))
+        def _():
+            pair_of[0].wait_recv()
+            pair_of[1].wait_send()
+
+        @pl.when(jnp.logical_not(bottom))
+        def _():
+            pair_of[1].wait_recv()
+            pair_of[0].wait_send()
+
+    for pair_of in halos:
+        start_halo(pair_of)
+
+    half = rows // 2
+    quarter = rows // 4
+    whole = [
+        (low - TILE, quarter), (low - TILE + quarter, quarter + TILE),
+        (low + 2 * quarter, quarter), (low + 3 * quarter, quarter + TILE),
+    ]
+    inner = [(low + quarter * j, quarter) for j in range(4)]
+    guess_parts = [(low, half), (low + half, half), (low - TILE, TILE), (high, TILE)]
+
+    def shift(stage, source, target, parts):
+        return [
+            tm_copy(
+                source(start, size), target.at[start:start + size],
+                ts_sem.at[stage, j], tr_sem.at[stage, j], later,
+            )
+            for j, (start, size) in enumerate(parts)
+        ]
+
+    def send(copy):
+        @pl.when(jnp.logical_not(last))
+        def _():
+            copy.start()
+
+    def receive(copy):
+        @pl.when(jnp.logical_not(first))
+        def _():
+            copy.wait_recv()
+
+    guess_shift = shift(
+        0,
+        lambda start, size: (
+            guess.at[1, start:start + size] if size == TILE else guess_in.at[1, start - low:start - low + size]
+        ),
+        guess_e, guess_parts,
+    )
+    v0_shift = shift(1, lambda start, size: v0.at[1, start:start + size], v0_e, whole)
+    v1_shift = shift(2, lambda start, size: v1.at[start:start + size], v1_e, whole)
+    v1f_shift = shift(3, lambda start, size: v1f.at[start:start + size], v1f_e, whole)
+    sol_shift = shift(4, lambda start, size: sol.at[1, start:start + size], sol_e, inner)
+    send(guess_shift[0])
+    send(guess_shift[1])
+
+    def blocks(start, size, step, init=None):
+        def run(i, carry):
+            return step(aligned(start + i * TILE), carry)
+
+        return lax.fori_loop(0, size // TILE, run, init)
+
+    @pl.when(first)
+    def _():
+        def clear(r, carry):
+            zero = jnp.zeros((TILE, width), jnp.float32)
+            for ref in (guess_e, v0_e, v1_e, v1f_e, sol_e):
+                ref[pl.ds(r, TILE), :] = zero
+            v2[1, pl.ds(r, TILE), :] = zero
+            return carry
+
+        blocks(low - TILE, rows + 2 * TILE, clear, 0)
+
+    def clear_edge(start):
+        for ref in (guess, rhs):
+            for p in range(2):
+                ref[p, start:start + TILE, :] = jnp.zeros((TILE, width), jnp.float32)
+        for p in range(2):
+            v2[p, start:start + TILE, :] = jnp.zeros((TILE, width), jnp.float32)
+        diff[start:start + TILE, :] = jnp.zeros((TILE, width), jnp.float32)
+
+    @pl.when(top)
+    def _():
+        clear_edge(low - TILE)
+
+    @pl.when(bottom)
+    def _():
+        clear_edge(high)
+
+    lane = lax.broadcasted_iota(jnp.int32, (TILE, width), 1)
+    not_left, not_right = lane != 0, lane != width - 1
+
+    def stencil(tall):
+        mid = tall[TILE:2 * TILE]
+        total = tall[TILE - 1:2 * TILE - 1] + tall[TILE + 1:2 * TILE + 1]
+        total = total + jnp.where(not_left, pltpu.roll(mid, 1, 1), 0.0)
+        total = total + jnp.where(not_right, pltpu.roll(mid, width - 1, 1), 0.0)
+        return mid, total
+
+    def tall_at(r):
+        return pl.ds(aligned(r - TILE), 3 * TILE)
+
+    def at(r):
+        return pl.ds(r, TILE)
+
+    def coefficients(level, r):
+        scaled = 2.0**level * diff[at(r), :]
+        diag = 1.0 + 4.0 * scaled
+        return scaled, diag, damping / diag
+
+    def squares(value, keep=None):
+        square = value * value
+        if keep is not None:
+            square = jnp.where(keep, square, 0.0)
+        total = square[:, 0:128]
+        for i in range(1, width // 128):
+            total = total + square[:, i * 128:(i + 1) * 128]
+        return total
+
+    zero_tile = jnp.zeros((TILE, 128), jnp.float32)
+    keep_share = 1.0 - damping
+
+    loads[0].wait()
+    loads[1].wait()
+    finish_halo(halos[0])
+    finish_halo(halos[1])
+    send(guess_shift[2])
+    send(guess_shift[3])
+    loads[2].wait()
+    finish_halo(halos[2])
+
+    def sweep_last(r, carry):
+        scaled, _, weight = coefficients(0, r)
+        mid, total = stencil(guess[1, tall_at(r), :])
+        v0[1, at(r), :] = keep_share * mid + weight * (rhs[1, at(r), :] + scaled * total + guess[0, at(r), :])
+        return carry
+
+    for (start, size), copy in zip(whole, v0_shift):
+        blocks(start, size, sweep_last, 0)
+        send(copy)
+
+    def sweep_first(r, carry):
+        scaled, _, weight = coefficients(0, r)
+        mid, total = stencil(guess[0, tall_at(r), :])
+        v0[0, at(r), :] = keep_share * mid + weight * (rhs[0, at(r), :] + scaled * total + guess_e[at(r), :])
+        return carry
+
+    for copy in guess_shift:
+        receive(copy)
+    blocks(low - TILE, rows + 2 * TILE, sweep_first, 0)
+
+    def descend(r, carry):
+        keep = jnp.logical_and(r >= low, r < high)
+        scaled, diag, _ = coefficients(0, r)
+        mid, total = stencil(v0[0, tall_at(r), :])
+        one = rhs[0, at(r), :] - diag * mid + scaled * total + v0_e[at(r), :]
+        late, total = stencil(v0[1, tall_at(r), :])
+        two = rhs[1, at(r), :] - diag * late + scaled * total + mid
+        source = one + two
+        g1[at(r), :] = source
+        _, _, weight = coefficients(1, r)
+        v1[at(r), :] = weight * source
+        return carry + squares(one, keep) + squares(two, keep)
+
+    total0 = zero_tile
+    for (start, size), arrived, copy in zip(whole, v0_shift, v1_shift):
+        receive(arrived)
+        total0 = blocks(start, size, descend, total0)
+        send(copy)
+
+    def residual1(r, carry):
+        keep = jnp.logical_and(r >= low, r < high)
+        scaled, _, _ = coefficients(1, r)
+        _, total = stencil(v1[tall_at(r), :])
+        resid = keep_share * g1[at(r), :] + scaled * total + v1_e[at(r), :]
+        r1[at(r), :] = resid
+        return carry + squares(resid, keep)
+
+    total1 = zero_tile
+    for (start, size), arrived in zip(whole, v1_shift):
+        receive(arrived)
+        total1 = blocks(start, size, residual1, total1)
+
+    mine = aligned(low - TILE + core * half)
+    theirs = aligned(low - TILE + (1 - core) * half)
+    span = half + 2 * TILE
+    swap = tm_copy(
+        r1.at[pl.ds(theirs, span)], pair.at[pl.ds(theirs, span)], ps_sem, pr_sem, me + 1 - 2 * core
+    )
+    swap.start()
+    swap_in = tm_copy(r1.at[pl.ds(mine, span)], pair.at[pl.ds(mine, span)], ps_sem, pr_sem, me + 1 - 2 * core)
+    swap_in.wait_recv()
+
+    def join(r, carry):
+        g2h[at(r), :] = r1[at(r), :] + pair[at(r), :]
+        return carry
+
+    blocks(mine, span, join, 0)
+    tall_piece = piece + 2 * TILE
+    c_low, c_high = EDGE, EDGE + piece
+    c_rows = slice(c_low - TILE, c_high + TILE)
+    for i in range(chips):
+        owner = core * chips + i
+        src = g2h.at[pl.ds(aligned(low - TILE + owner * piece), tall_piece)]
+        copy = tm_copy(src, c_g2.at[chip, c_rows], as_sem.at[i], ar_sem.at[chip], owner)
+        local = pltpu.make_async_copy(src, c_g2.at[chip, c_rows], al_sem)
+
+        @pl.when(owner == me)
+        def _():
+            local.start()
+            local.wait()
+
+        @pl.when(owner != me)
+        def _():
+            copy.start()
+
+    giver = me // chips
+    for c in range(chips):
+        copy = tm_copy(
+            g2h.at[pl.ds(low, tall_piece)], c_g2.at[c, c_rows], as_sem.at[0], ar_sem.at[c],
+            lax.rem(me + 1, devices),
+        )
+
+        @pl.when(2 * c + giver != me)
+        def _():
+            copy.wait_recv()
+
+    offset = me * piece
+
+    def coarse_coefficients(level, r):
+        return coefficients(level, aligned(r + offset))
+
+    def coarse(step, init=0):
+        return blocks(c_low - TILE, tall_piece, step, init)
+
+    def first_sweep(level, source, field, count):
+        def step(r, carry):
+            _, _, weight = coarse_coefficients(level, r)
+            for p in range(count):
+                field[p, at(r), :] = weight * source[p, at(r), :]
+            return carry
+
+        coarse(step)
+
+    def coarse_residual(level, source, field, target, count):
+        def step(r, carry):
+            keep = jnp.logical_and(r >= c_low, r < c_high)
+            scaled, _, _ = coarse_coefficients(level, r)
+            earlier, even = None, None
+            for p in range(count):
+                mid, total = stencil(field[p, tall_at(r), :])
+                resid = keep_share * source[p, at(r), :] + scaled * total
+                if p:
+                    resid = resid + earlier
+                earlier = mid
+                carry = carry + squares(resid, keep)
+                if p % 2 == 0:
+                    even = resid
+                else:
+                    target[p // 2, at(r), :] = even + resid
+            return carry
+
+        return coarse(step, zero_tile)
+
+    def ascend(level, source, field, above, target, count):
+        def step(r, carry):
+            scaled, _, weight = coarse_coefficients(level, r)
+            earlier = None
+            for p in range(count):
+                mid, total = stencil(field[p, tall_at(r), :] + above[p // 2, tall_at(r), :])
+                value = source[p, at(r), :] + scaled * total
+                if p:
+                    value = value + earlier
+                earlier = mid
+                target[p, at(r), :] = keep_share * mid + weight * value
+            return carry
+
+        coarse(step)
+
+    points2, points3 = chips, chips // 2
+    first_sweep(2, c_g2, c_v2, points2)
+    total2 = coarse_residual(2, c_g2, c_v2, c_g3, points2)
+    first_sweep(3, c_g3, c_v3, points3)
+    total3 = coarse_residual(3, c_g3, c_v3, c_g4, points3)
+    first_sweep(4, c_g4, c_v4, 1)
+
+    def second_sweep(r, carry):
+        scaled, _, weight = coarse_coefficients(4, r)
+        mid, total = stencil(c_v4[0, tall_at(r), :])
+        c_v4b[0, at(r), :] = keep_share * mid + weight * (c_g4[0, at(r), :] + scaled * total)
+        return carry
+
+    coarse(second_sweep)
+
+    def residual4(r, carry):
+        scaled, diag, _ = coarse_coefficients(4, r)
+        mid, total = stencil(c_v4b[0, tall_at(r), :])
+        return carry + squares(c_g4[0, at(r), :] - diag * mid + scaled * total)
+
+    total4 = blocks(c_low, piece, residual4, zero_tile)
+    c_v3f, c_v2f = acc
+    ascend(3, c_g3, c_v3, c_v4b, c_v3f, points3)
+    ascend(2, c_g2, c_v2, c_v3f, c_v2f, points2)
+
+    back = []
+    place = pl.ds(aligned(low + offset), piece)
+    for j in range(devices):
+        wants = [(0, j // 2)]
+        if j % 2 == 0 and j > 0:
+            wants.append((1, j // 2 - 1))
+        for kind, point in wants:
+            src, dst = c_v2f.at[point, c_low:c_high], v2.at[kind, place]
+            copy = tm_copy(src, dst, bs_sem.at[kind, j], br_sem.at[kind, me], j)
+            local = pltpu.make_async_copy(src, dst, bl_sem.at[kind])
+            back.append((j, copy))
+
+            @pl.when(me == j)
+            def _():
+                local.start()
+                local.wait()
+
+            @pl.when(me != j)
+            def _():
+                copy.start()
+
+    has_second = jnp.logical_and(core == 0, jnp.logical_not(first))
+    for kind in range(2):
+        for k in range(devices):
+            copy = tm_copy(
+                c_v2f.at[0, c_low:c_high], v2.at[kind, low + k * piece:low + (k + 1) * piece],
+                bs_sem.at[kind, 0], br_sem.at[kind, k], lax.rem(me + 1, devices),
+            )
+            needed = me != k
+            if kind:
+                needed = jnp.logical_and(needed, has_second)
+
+            @pl.when(needed)
+            def _():
+                copy.wait_recv()
+
+    v2_halos = [
+        halo_pair(
+            3 + kind, v2.at[kind, high - TILE:high], v2.at[kind, low:low + TILE],
+            v2.at[kind, before_low], v2.at[kind, after_high],
+        )
+        for kind in range(2)
+    ]
+    start_halo(v2_halos[0])
+
+    @pl.when(has_second)
+    def _():
+        start_halo(v2_halos[1])
+
+    finish_halo(v2_halos[0])
+
+    @pl.when(has_second)
+    def _():
+        finish_halo(v2_halos[1])
+
+    kind = 1 - core
+
+    def ascend1(r, carry):
+        scaled, _, weight = coefficients(1, r)
+        mid, total = stencil(v1[tall_at(r), :] + v2[0, tall_at(r), :])
+        earlier = v1_e[at(r), :] + v2[kind, at(r), :]
+        v1f[at(r), :] = keep_share * mid + weight * (g1[at(r), :] + scaled * total + earlier)
+        return carry
+
+    for (start, size), copy in zip(whole, v1f_shift):
+        blocks(start, size, ascend1, 0)
+        send(copy)
+
+    def ascend_last(r, carry):
+        scaled, _, weight = coefficients(0, r)
+        mid, total = stencil(v0[1, tall_at(r), :] + v1f[tall_at(r), :])
+        earlier = v0[0, at(r), :] + v1f[at(r), :]
+        sol[1, at(r), :] = keep_share * mid + weight * (rhs[1, at(r), :] + scaled * total + earlier)
+        return carry
+
+    blocks(low - TILE, TILE, ascend_last, 0)
+    for (start, size), copy in zip(inner, sol_shift):
+        blocks(start, size, ascend_last, 0)
+        send(copy)
+    blocks(high, TILE, ascend_last, 0)
+
+    def ascend_first(r, carry):
+        scaled, _, weight = coefficients(0, r)
+        mid, total = stencil(v0[0, tall_at(r), :] + v1f[tall_at(r), :])
+        earlier = v0_e[at(r), :] + v1f_e[at(r), :]
+        sol[0, at(r), :] = keep_share * mid + weight * (rhs[0, at(r), :] + scaled * total + earlier)
+        return carry
+
+    for (start, size), arrived in zip(whole, v1f_shift):
+        receive(arrived)
+        blocks(start, size, ascend_first, 0)
+    stores = pltpu.make_async_copy(sol.at[:, low:high], out, store_sem)
+    stores.start()
+
+    def final_last(r, carry):
+        scaled, diag, _ = coefficients(0, r)
+        mid, total = stencil(sol[1, tall_at(r), :])
+        return carry + squares(rhs[1, at(r), :] - diag * mid + scaled * total + sol[0, at(r), :])
+
+    total5 = blocks(low, rows, final_last, zero_tile)
+
+    def final_first(r, carry):
+        scaled, diag, _ = coefficients(0, r)
+        mid, total = stencil(sol[0, tall_at(r), :])
+        return carry + squares(rhs[0, at(r), :] - diag * mid + scaled * total + sol_e[at(r), :])
+
+    for (start, size), arrived in zip(inner, sol_shift):
+        receive(arrived)
+        total5 = blocks(start, size, final_first, total5)
+
+    parts = [total0, total1, total2, total3, total4, total5]
+    for level, value in enumerate(parts):
+        tile[level:level + 1, :] = jnp.sum(value, axis=0, keepdims=True)
+    for level in range(len(parts), TILE):
+        tile[level:level + 1, :] = jnp.zeros((1, 128), jnp.float32)
+
+    def exchange(count, own, source, slots, copier, send_sems, recv_sems):
+        slots[pl.ds(own, 1)] = source[...][None]
+        sent = [
+            copier(source, slots.at[own], send_sems.at[i], recv_sems.at[own], lax.rem(own + i, count))
+            for i in range(1, count)
+        ]
+        for copy in sent:
+            copy.start()
+        for i in range(1, count):
+            other = lax.rem(own + i, count)
+            copier(source, slots.at[other], send_sems.at[i], recv_sems.at[other], other).wait_recv()
+        for copy in sent:
+            copy.wait_send()
+        total = slots[0]
+        for i in range(1, count):
+            total = total + slots[i]
+        return total
+
+    total = exchange(devices, me, tile, gathered, tm_copy, ns_sem, nr_sem)
+    tile[...] = total
+    total = exchange(strips, strip, tile, gathered_z, space_copy, ms_sem, mr_sem)
+    summed = jnp.sum(total, axis=1, keepdims=True)
+    norms_out[...] = jnp.broadcast_to(jnp.sqrt(summed * (1.0 / cells)), (TILE, 128))
+
+    stores.wait()
+    for group in (guess_shift, v0_shift, v1_shift, v1f_shift, sol_shift):
+        for copy in group:
+            @pl.when(jnp.logical_not(last))
+            def _():
+                copy.wait_send()
+    swap.wait_send()
+    for i in range(chips):
+        owner = core * chips + i
+        copy = tm_copy(
+            g2h.at[pl.ds(aligned(low - TILE + owner * piece), tall_piece)], c_g2.at[chip, c_rows],
+            as_sem.at[i], ar_sem.at[chip], owner,
+        )
+
+        @pl.when(owner != me)
+        def _():
+            copy.wait_send()
+    for j, copy in back:
+        @pl.when(me != j)
+        def _():
+            copy.wait_send()
+
+
+def fast_body(rhs, guess, diffusion):
+    devices, strips = lax.axis_size("tm"), lax.axis_size("space")
+    rows, width = rhs.shape[1:]
+    chips = devices // 2
+    cells = rows * strips * width
+    height = rows + 2 * EDGE
+    c_height = rows // devices + 2 * EDGE
+
+    def plane(*lead):
+        return pltpu.VMEM(lead + (height, width), jnp.float32)
+
+    def coarse(count):
+        return pltpu.VMEM((count, c_height, width), jnp.float32)
+
+    dma = pltpu.SemaphoreType.DMA
+    scratch = [
+        plane(2), plane(2), plane(), plane(2), plane(), plane(), plane(), plane(), plane(2),
+        plane(), plane(), plane(), plane(), plane(),
+        plane(), plane(), plane(2),
+        coarse(chips), coarse(chips), coarse(chips // 2), coarse(chips // 2), coarse(1), coarse(1), coarse(1),
+        (coarse(chips // 2), coarse(chips)),
+        pltpu.VMEM((TILE, 128), jnp.float32),
+        pltpu.VMEM((devices, TILE, 128), jnp.float32),
+        pltpu.VMEM((strips, TILE, 128), jnp.float32),
+        dma((3,)), dma, dma((5, 2)), dma((5, 2)), dma((5, 4)), dma((5, 4)), dma, dma,
+        dma((chips,)), dma((chips,)), dma, dma((2, devices)), dma((2, devices)), dma((2,)),
+        dma((devices,)), dma((devices,)), dma((strips,)), dma((strips,)),
+    ]
+    any_space = pl.BlockSpec(memory_space=pl.ANY)
+    result, norms = pl.pallas_call(
+        functools.partial(cycle_kernel, strips, devices, cells),
+        out_shape=(
+            jax.ShapeDtypeStruct(rhs.shape, jnp.float32),
+            jax.ShapeDtypeStruct((TILE, 128), jnp.float32),
+        ),
+        in_specs=[any_space] * 3,
+        out_specs=(any_space, pl.BlockSpec(memory_space=pltpu.VMEM)),
+        scratch_shapes=scratch,
+        compiler_params=pltpu.CompilerParams(
+            collective_id=0, has_side_effects=True, vmem_limit_bytes=60 * 2**20
+        ),
+    )(rhs, guess, diffusion)
+    return result, norms[:LEVELS + 1, 0]
+
+
 def solution(mesh):
     in_specs = (P("tm", "space", None), P("tm", "space", None), P("space", None))
     out_specs = (P("tm", "space", None), P())
-    return jax.shard_map(body, mesh=mesh, in_specs=in_specs, out_specs=out_specs, check_vma=False)
+
+    def choose(rhs, guess, diffusion):
+        points = rhs.shape[0] * lax.axis_size("tm")
+        one_coarsest = points == 2 ** (LEVELS - 1) and rhs.shape[0] == 2
+        even = rhs.shape[1] % (TILE * lax.axis_size("tm")) == 0 and rhs.shape[2] % 128 == 0
+        if one_coarsest and even:
+            return fast_body(rhs, guess, diffusion)
+        return body(rhs, guess, diffusion)
+
+    return jax.shard_map(choose, mesh=mesh, in_specs=in_specs, out_specs=out_specs, check_vma=False)

time: 331 us -> 122 us (0.37)
  starting transfers between devices: 136 us -> 0 us
  Pallas kernels: 0 us -> 116 us
  waiting for transfers between devices: 106 us -> 0 us
  blocking collectives: 44.9 us -> 0 us
  other arithmetic: 30.2 us -> 0 us
  local copies, waits for them, and re-layouts: 9.38 us -> 4.47 us
    ppermute x39 -> x0, starting transfers between devices: 136 us -> none  [the longest x12 56 us: with_halo(): lax.ppermute(lax.slice_in_dim(block, block.shape[dim] - width, None, axis...]
    pallas_call x0 -> x1, Pallas kernels: none -> 116 us  [fast_body(): pl.pallas_call(functools.partial(cycle_kernel, strips, devices, cells), o...]
    ppermute x39 -> x0, waiting for transfers between devices: 106 us -> none  [the longest x12 48.7 us: shifted(): lax.ppermute(value, axis, [(source, source + steps) for source in range(f...]
    psum x1 -> x0, blocking collectives: 44.9 us -> none  [body(): totals = lax.psum(jnp.stack(partials), ('tm', 'space'))]
    reduce_sum x6 -> x0, other arithmetic: 11.6 us -> none  [record(): local_part = jnp.sum(resid * resid) * weight_of(level)]
    add x8 -> x0, other arithmetic: 10.2 us -> none  [the longest x5 5.33 us: body(): field = fields[level] + correction]
    concatenate x12 -> x0, other arithmetic: 6.46 us -> none  [with_halo(): block = jnp.concatenate([low, block, high], axis=dim)]
    slice x16 -> x1, local copies, waits for them, and re-layouts: 5.99 us -> 1.31 us  [fast_body(): return (result, norms[:LEVELS + 1, 0])]
  transfers between devices with their start and end apart: 39 -> 0, of which waited for: 16 -> 0; matrix products, arithmetic and copies ran while one was open for 4% -> 0% of each run, Pallas kernels for 0% -> 0%
where the time goes in v1:
time: 122 us
  Pallas kernels  116 us (95%)
  local copies, waits for them, and re-layouts  4.47 us (4%)
    pallas_call x1, Pallas kernels, fast_body(): pl.pallas_call(functools.partial(cycle_kernel, strips, devices, cells), o...  116 us
    unnamed x1, local copies, waits for them, and re-layouts  3.16 us

profile of v1, /device:TPU:0, one launch (start us, length us, event | category | flops | bytes accessed | tf_op | source)
XLA Modules:
  0.0 121.6 jit_solution(16216693685863904193)
XLA Ops:
  0.6 116.4 %shard_map.50 = (f32[2,256,1024]{2,1,0:T(8,128)}, f32[8,128]{1,0:T(8,128)}) custom-call(f32[2,256,1024]{2,1,0:T(8,128)} %rhs_in.1, f32[2,256,1024]{2,1,0:T(8,128)} %guess_in.1, f32[256,1024]{1,0:T(8,128)} %diff_in.1), custom_call_target="tpu_custom_call" | custom-call | tf_op jit(solution)/shard_map/pallas_call | solution.py:711
  117.1 1.3 %slice_reduce_fusion = f32[6]{0:T(128)} fusion(f32[8,128]{1,0:T(8,128)} %get-tuple-element.5), kind=kLoop, calls=%fused_computation | loop fusion | bytes 48 | tf_op jit(solution)/shard_map/slice | solution.py:724
  118.4 3.2 %copy.6 = f32[2,256,1024]{2,1,0:T(8,128)} copy(f32[2,256,1024]{2,1,0:T(8,128)} %get-tuple-element.8) | data formatting | bytes 4194304

commit v2 on v1

--- a/solution.py
+++ b/solution.py
@@ -128,10 +128,10 @@
 def cycle_kernel(
     strips, devices, cells,
     rhs_in, guess_in, diff_in, out, norms_out,
-    rhs, guess, diff, v0, g1, v1, r1, v1f, sol, guess_e, v0_e, v1_e, v1f_e, sol_e,
+    rhs, guess, diff, v0, g1, v1, r1, v1f, sol, guess_e, v0_e, v1_e, v1_ee, v1f_e, sol_e,
     pair, g2h, v2, c_g2, c_v2, c_g3, c_v3, c_g4, c_v4, c_v4b, acc, tile, gathered, gathered_z,
     load_sem, store_sem, zs_sem, zr_sem, ts_sem, tr_sem, ps_sem, pr_sem, as_sem, ar_sem, al_sem,
-    bs_sem, br_sem, bl_sem, ns_sem, nr_sem, ms_sem, mr_sem,
+    bs_sem, br_sem, bl_sem, rs_sem, es_sem, er_sem, ns_sem, nr_sem, ms_sem, mr_sem,
 ):
     me = lax.axis_index("tm")
     strip = lax.axis_index("space")
@@ -278,7 +278,7 @@
     def _():
         def clear(r, carry):
             zero = jnp.zeros((TILE, width), jnp.float32)
-            for ref in (guess_e, v0_e, v1_e, v1f_e, sol_e):
+            for ref in (guess_e, v0_e, v1_e, v1_ee, v1f_e, sol_e):
                 ref[pl.ds(r, TILE), :] = zero
             v2[1, pl.ds(r, TILE), :] = zero
             return carry
@@ -438,6 +438,21 @@
         @pl.when(2 * c + giver != me)
         def _():
             copy.wait_recv()
+
+    skip_shift = [
+        tm_copy(
+            v1.at[start:start + size], v1_ee.at[start:start + size], es_sem.at[j], er_sem.at[j],
+            jnp.minimum(me + 2, devices - 1),
+        )
+        for j, (start, size) in enumerate(whole)
+    ]
+    sends_skip = jnp.logical_and(core == 0, chip < chips - 1)
+    has_second = jnp.logical_and(core == 0, jnp.logical_not(first))
+
+    @pl.when(sends_skip)
+    def _():
+        for copy in skip_shift:
+            copy.start()
 
     offset = me * piece
 
@@ -518,39 +533,48 @@
 
     back = []
     place = pl.ds(aligned(low + offset), piece)
-    for j in range(devices):
-        wants = [(0, j // 2)]
-        if j % 2 == 0 and j > 0:
-            wants.append((1, j // 2 - 1))
-        for kind, point in wants:
+    for c in range(chips):
+        wants = [(0, 2 * c + core, c)]
+        if c > 0:
+            wants.append((1, 2 * c, c - 1))
+        for kind, target, point in wants:
             src, dst = c_v2f.at[point, c_low:c_high], v2.at[kind, place]
-            copy = tm_copy(src, dst, bs_sem.at[kind, j], br_sem.at[kind, me], j)
+            copy = tm_copy(src, dst, bs_sem.at[kind, c], br_sem.at[kind, me], target)
             local = pltpu.make_async_copy(src, dst, bl_sem.at[kind])
-            back.append((j, copy))
-
-            @pl.when(me == j)
+            back.append((target, copy))
+
+            @pl.when(me == target)
             def _():
                 local.start()
                 local.wait()
 
-            @pl.when(me != j)
+            @pl.when(me != target)
             def _():
                 copy.start()
 
-    has_second = jnp.logical_and(core == 0, jnp.logical_not(first))
-    for kind in range(2):
-        for k in range(devices):
-            copy = tm_copy(
-                c_v2f.at[0, c_low:c_high], v2.at[kind, low + k * piece:low + (k + 1) * piece],
-                bs_sem.at[kind, 0], br_sem.at[kind, k], lax.rem(me + 1, devices),
-            )
-            needed = me != k
-            if kind:
-                needed = jnp.logical_and(needed, has_second)
-
-            @pl.when(needed)
-            def _():
-                copy.wait_recv()
+    sibling = me + 1 - 2 * core
+    relays = []
+    for i in range(chips):
+        for side in (core, 1 - core):
+            k = 2 * i + side
+            rows_of = pl.ds(aligned(low + k * piece), piece)
+            arrival = tm_copy(v2.at[0, rows_of], v2.at[0, rows_of], rs_sem.at[i], br_sem.at[0, k], sibling)
+            relays.append((k, arrival))
+    for k, arrival in relays[0::2]:
+        @pl.when(k != me)
+        def _():
+            arrival.wait_recv()
+
+        arrival.start()
+    for k, arrival in relays[1::2]:
+        arrival.wait_recv()
+    for k in range(devices):
+        rows_of = slice(low + k * piece, low + (k + 1) * piece)
+        arrival = tm_copy(v2.at[1, rows_of], v2.at[1, rows_of], bs_sem.at[1, 0], br_sem.at[1, k], sibling)
+
+        @pl.when(jnp.logical_and(k != me, has_second))
+        def _():
+            arrival.wait_recv()
 
     v2_halos = [
         halo_pair(
@@ -582,7 +606,10 @@
 
     for (start, size), copy in zip(whole, v1f_shift):
         blocks(start, size, ascend1, 0)
-        send(copy)
+
+        @pl.when(core == 0)
+        def _():
+            copy.start()
 
     def ascend_last(r, carry):
         scaled, _, weight = coefficients(0, r)
@@ -604,8 +631,23 @@
         sol[0, at(r), :] = keep_share * mid + weight * (rhs[0, at(r), :] + scaled * total + earlier)
         return carry
 
-    for (start, size), arrived in zip(whole, v1f_shift):
-        receive(arrived)
+    def ascend_before(r, carry):
+        scaled, _, weight = coefficients(1, r)
+        early, above = v1_e[at(r), :], v2[1, at(r), :]
+        mid, total = stencil(v1_e[tall_at(r), :] + v2[1, tall_at(r), :])
+        v1f_e[at(r), :] = keep_share * mid + early + weight * (scaled * total + v1_ee[at(r), :] + above)
+        return carry
+
+    for (start, size), arrived, skipped in zip(whole, v1f_shift, skip_shift):
+        @pl.when(core == 1)
+        def _():
+            arrived.wait_recv()
+
+        @pl.when(has_second)
+        def _():
+            skipped.wait_recv()
+            blocks(start, size, ascend_before, 0)
+
         blocks(start, size, ascend_first, 0)
     stores = pltpu.make_async_copy(sol.at[:, low:high], out, store_sem)
     stores.start()
@@ -657,11 +699,21 @@
     norms_out[...] = jnp.broadcast_to(jnp.sqrt(summed * (1.0 / cells)), (TILE, 128))
 
     stores.wait()
-    for group in (guess_shift, v0_shift, v1_shift, v1f_shift, sol_shift):
+    for group in (guess_shift, v0_shift, v1_shift, sol_shift):
         for copy in group:
             @pl.when(jnp.logical_not(last))
             def _():
                 copy.wait_send()
+    for copy in v1f_shift:
+        @pl.when(core == 0)
+        def _():
+            copy.wait_send()
+    for copy in skip_shift:
+        @pl.when(sends_skip)
+        def _():
+            copy.wait_send()
+    for _, copy in relays[0::2]:
+        copy.wait_send()
     swap.wait_send()
     for i in range(chips):
         owner = core * chips + i
@@ -673,8 +725,8 @@
         @pl.when(owner != me)
         def _():
             copy.wait_send()
-    for j, copy in back:
-        @pl.when(me != j)
+    for target, copy in back:
+        @pl.when(me != target)
         def _():
             copy.wait_send()
 
@@ -696,7 +748,7 @@
     dma = pltpu.SemaphoreType.DMA
     scratch = [
         plane(2), plane(2), plane(), plane(2), plane(), plane(), plane(), plane(), plane(2),
-        plane(), plane(), plane(), plane(), plane(),
+        plane(), plane(), plane(), plane(), plane(), plane(),
         plane(), plane(), plane(2),
         coarse(chips), coarse(chips), coarse(chips // 2), coarse(chips // 2), coarse(1), coarse(1), coarse(1),
         (coarse(chips // 2), coarse(chips)),
@@ -705,6 +757,7 @@
         pltpu.VMEM((strips, TILE, 128), jnp.float32),
         dma((3,)), dma, dma((5, 2)), dma((5, 2)), dma((5, 4)), dma((5, 4)), dma, dma,
         dma((chips,)), dma((chips,)), dma, dma((2, devices)), dma((2, devices)), dma((2,)),
+        dma((chips,)), dma((4,)), dma((4,)),
         dma((devices,)), dma((devices,)), dma((strips,)), dma((strips,)),
     ]
     any_space = pl.BlockSpec(memory_space=pl.ANY)

time: 122 us -> 120 us (0.984)
    pallas_call x1, Pallas kernels: 116 us -> 115 us  [fast_body(): pl.pallas_call(functools.partial(cycle_kernel, strips, devices, cells), o...]
where the time goes in v2:
time: 120 us
  Pallas kernels  115 us (96%)
  local copies, waits for them, and re-layouts  4.47 us (4%)
    pallas_call x1, Pallas kernels, fast_body(): pl.pallas_call(functools.partial(cycle_kernel, strips, devices, cells), o...  115 us
    unnamed x1, local copies, waits for them, and re-layouts  3.16 us

profile of v2, /device:TPU:0, one launch (start us, length us, event | category | flops | bytes accessed | tf_op | source)
XLA Modules:
  0.0 119.6 jit_solution(4339253880251521925)
XLA Ops:
  0.6 114.5 %shard_map.50 = (f32[2,256,1024]{2,1,0:T(8,128)}, f32[8,128]{1,0:T(8,128)}) custom-call(f32[2,256,1024]{2,1,0:T(8,128)} %rhs_in.1, f32[2,256,1024]{2,1,0:T(8,128)} %guess_in.1, f32[256,1024]{1,0:T(8,128)} %diff_in.1), custom_call_target="tpu_custom_call" | custom-call | tf_op jit(solution)/shard_map/pallas_call | solution.py:764
  115.2 1.3 %slice_reduce_fusion = f32[6]{0:T(128)} fusion(f32[8,128]{1,0:T(8,128)} %get-tuple-element.5), kind=kLoop, calls=%fused_computation | loop fusion | bytes 48 | tf_op jit(solution)/shard_map/slice | solution.py:777
  116.5 3.2 %copy.6 = f32[2,256,1024]{2,1,0:T(8,128)} copy(f32[2,256,1024]{2,1,0:T(8,128)} %get-tuple-element.8) | data formatting | bytes 4194304

commit v3 on v2

--- a/solution.py
+++ b/solution.py
@@ -123,13 +123,14 @@
 DEVICE = pl.DeviceIdType.MESH
 TILE = 8
 EDGE = 2 * TILE
+BLOCK = 32
 
 
 def cycle_kernel(
     strips, devices, cells,
     rhs_in, guess_in, diff_in, out, norms_out,
     rhs, guess, diff, v0, g1, v1, r1, v1f, sol, guess_e, v0_e, v1_e, v1_ee, v1f_e, sol_e,
-    pair, g2h, v2, c_g2, c_v2, c_g3, c_v3, c_g4, c_v4, c_v4b, acc, tile, gathered, gathered_z,
+    pair, g2h, v2, c_g2, c_v2, c_g3, c_v3, c_g4, c_v4, c_v4b, finals, weights, tile, gathered, gathered_z,
     load_sem, store_sem, zs_sem, zr_sem, ts_sem, tr_sem, ps_sem, pr_sem, as_sem, ar_sem, al_sem,
     bs_sem, br_sem, bl_sem, rs_sem, es_sem, er_sem, ns_sem, nr_sem, ms_sem, mr_sem,
 ):
@@ -229,7 +230,7 @@
     half = rows // 2
     quarter = rows // 4
     whole = [
-        (low - TILE, quarter), (low - TILE + quarter, quarter + TILE),
+        (low - TILE, quarter + TILE), (low + quarter, quarter),
         (low + 2 * quarter, quarter), (low + 3 * quarter, quarter + TILE),
     ]
     inner = [(low + quarter * j, quarter) for j in range(4)]
@@ -268,22 +269,44 @@
     send(guess_shift[0])
     send(guess_shift[1])
 
-    def blocks(start, size, step, init=None):
-        def run(i, carry):
-            return step(aligned(start + i * TILE), carry)
-
-        return lax.fori_loop(0, size // TILE, run, init)
+    block = [TILE]
+
+    def at(r):
+        return pl.ds(r, block[0])
+
+    def blocks(start, size, step, init=0, ahead=0):
+        def loop(begin, count, tall, carry):
+            def run(i, carry):
+                return step(aligned(begin + i * tall), carry)
+
+            block[0] = tall
+            if count == 1:
+                carry = step(aligned(begin), carry)
+            elif count:
+                carry = lax.fori_loop(0, count, run, carry)
+            block[0] = TILE
+            return carry
+
+        carry = loop(start, ahead // TILE, TILE, init)
+        count = (size - ahead) // BLOCK
+        carry = loop(start + ahead, count, BLOCK, carry)
+        done = ahead + count * BLOCK
+        return loop(start + done, (size - done) // TILE, TILE, carry)
 
     @pl.when(first)
     def _():
         def clear(r, carry):
-            zero = jnp.zeros((TILE, width), jnp.float32)
+            zero = jnp.zeros((block[0], width), jnp.float32)
             for ref in (guess_e, v0_e, v1_e, v1_ee, v1f_e, sol_e):
-                ref[pl.ds(r, TILE), :] = zero
-            v2[1, pl.ds(r, TILE), :] = zero
+                ref[at(r), :] = zero
+            v2[1, at(r), :] = zero
             return carry
 
-        blocks(low - TILE, rows + 2 * TILE, clear, 0)
+        blocks(low - TILE, rows + 2 * TILE, clear, 0, TILE)
+
+    def chunk(j, step, init=0):
+        start, size = whole[j]
+        return blocks(start, size, step, init, TILE if j == 0 else 0)
 
     def clear_edge(start):
         for ref in (guess, rhs):
@@ -301,26 +324,30 @@
     def _():
         clear_edge(high)
 
-    lane = lax.broadcasted_iota(jnp.int32, (TILE, width), 1)
-    not_left, not_right = lane != 0, lane != width - 1
-
     def stencil(tall):
-        mid = tall[TILE:2 * TILE]
-        total = tall[TILE - 1:2 * TILE - 1] + tall[TILE + 1:2 * TILE + 1]
+        size = block[0]
+        lane = lax.broadcasted_iota(jnp.int32, (size, width), 1)
+        not_left, not_right = lane != 0, lane != width - 1
+        mid = tall[TILE:TILE + size]
+        total = tall[TILE - 1:TILE + size - 1] + tall[TILE + 1:TILE + size + 1]
         total = total + jnp.where(not_left, pltpu.roll(mid, 1, 1), 0.0)
         total = total + jnp.where(not_right, pltpu.roll(mid, width - 1, 1), 0.0)
         return mid, total
 
     def tall_at(r):
-        return pl.ds(aligned(r - TILE), 3 * TILE)
-
-    def at(r):
-        return pl.ds(r, TILE)
+        return pl.ds(aligned(r - TILE), block[0] + 2 * TILE)
 
     def coefficients(level, r):
         scaled = 2.0**level * diff[at(r), :]
         diag = 1.0 + 4.0 * scaled
+        if level < 2:
+            return scaled, diag, weights[level, at(r), :]
         return scaled, diag, damping / diag
+
+    def set_weights(r, carry):
+        for level in range(2):
+            weights[level, at(r), :] = damping / (1.0 + 4.0 * (2.0**level * diff[at(r), :]))
+        return carry
 
     def squares(value, keep=None):
         square = value * value
@@ -329,19 +356,13 @@
         total = square[:, 0:128]
         for i in range(1, width // 128):
             total = total + square[:, i * 128:(i + 1) * 128]
-        return total
+        folded = total[0:TILE]
+        for i in range(TILE, block[0], TILE):
+            folded = folded + total[i:i + TILE]
+        return folded
 
     zero_tile = jnp.zeros((TILE, 128), jnp.float32)
     keep_share = 1.0 - damping
-
-    loads[0].wait()
-    loads[1].wait()
-    finish_halo(halos[0])
-    finish_halo(halos[1])
-    send(guess_shift[2])
-    send(guess_shift[3])
-    loads[2].wait()
-    finish_halo(halos[2])
 
     def sweep_last(r, carry):
         scaled, _, weight = coefficients(0, r)
@@ -349,9 +370,22 @@
         v0[1, at(r), :] = keep_share * mid + weight * (rhs[1, at(r), :] + scaled * total + guess[0, at(r), :])
         return carry
 
-    for (start, size), copy in zip(whole, v0_shift):
-        blocks(start, size, sweep_last, 0)
-        send(copy)
+    for copy in loads:
+        copy.wait()
+    blocks(low, rows, set_weights)
+    for j in (1, 2):
+        chunk(j, sweep_last)
+        send(v0_shift[j])
+    finish_halo(halos[0])
+    send(guess_shift[2])
+    send(guess_shift[3])
+    finish_halo(halos[1])
+    finish_halo(halos[2])
+    blocks(low - TILE, TILE, set_weights)
+    blocks(high, TILE, set_weights)
+    for j in (0, 3):
+        chunk(j, sweep_last)
+        send(v0_shift[j])
 
     def sweep_first(r, carry):
         scaled, _, weight = coefficients(0, r)
@@ -361,7 +395,8 @@
 
     for copy in guess_shift:
         receive(copy)
-    blocks(low - TILE, rows + 2 * TILE, sweep_first, 0)
+    for j in range(4):
+        chunk(j, sweep_first)
 
     def descend(r, carry):
         keep = jnp.logical_and(r >= low, r < high)
@@ -377,10 +412,10 @@
         return carry + squares(one, keep) + squares(two, keep)
 
     total0 = zero_tile
-    for (start, size), arrived, copy in zip(whole, v0_shift, v1_shift):
-        receive(arrived)
-        total0 = blocks(start, size, descend, total0)
-        send(copy)
+    for j in (1, 2, 0, 3):
+        receive(v0_shift[j])
+        total0 = chunk(j, descend, total0)
+        send(v1_shift[j])
 
     def residual1(r, carry):
         keep = jnp.logical_and(r >= low, r < high)
@@ -391,9 +426,9 @@
         return carry + squares(resid, keep)
 
     total1 = zero_tile
-    for (start, size), arrived in zip(whole, v1_shift):
-        receive(arrived)
-        total1 = blocks(start, size, residual1, total1)
+    for j in (1, 2, 0, 3):
+        receive(v1_shift[j])
+        total1 = chunk(j, residual1, total1)
 
     mine = aligned(low - TILE + core * half)
     theirs = aligned(low - TILE + (1 - core) * half)
@@ -409,7 +444,7 @@
         g2h[at(r), :] = r1[at(r), :] + pair[at(r), :]
         return carry
 
-    blocks(mine, span, join, 0)
+    blocks(mine, span, join, 0, TILE)
     tall_piece = piece + 2 * TILE
     c_low, c_high = EDGE, EDGE + piece
     c_rows = slice(c_low - TILE, c_high + TILE)
@@ -439,12 +474,13 @@
         def _():
             copy.wait_recv()
 
+    early_half = ()
     skip_shift = [
         tm_copy(
             v1.at[start:start + size], v1_ee.at[start:start + size], es_sem.at[j], er_sem.at[j],
             jnp.minimum(me + 2, devices - 1),
         )
-        for j, (start, size) in enumerate(whole)
+        for j, (start, size) in enumerate(whole) if j in early_half
     ]
     sends_skip = jnp.logical_and(core == 0, chip < chips - 1)
     has_second = jnp.logical_and(core == 0, jnp.logical_not(first))
@@ -459,8 +495,9 @@
     def coarse_coefficients(level, r):
         return coefficients(level, aligned(r + offset))
 
+
     def coarse(step, init=0):
-        return blocks(c_low - TILE, tall_piece, step, init)
+        return blocks(c_low - TILE, tall_piece, step, init, TILE)
 
     def first_sweep(level, source, field, count):
         def step(r, carry):
@@ -527,7 +564,7 @@
         return carry + squares(c_g4[0, at(r), :] - diag * mid + scaled * total)
 
     total4 = blocks(c_low, piece, residual4, zero_tile)
-    c_v3f, c_v2f = acc
+    c_v3f, c_v2f = finals
     ascend(3, c_g3, c_v3, c_v4b, c_v3f, points3)
     ascend(2, c_g2, c_v2, c_v3f, c_v2f, points2)
 
@@ -589,12 +626,6 @@
     def _():
         start_halo(v2_halos[1])
 
-    finish_halo(v2_halos[0])
-
-    @pl.when(has_second)
-    def _():
-        finish_halo(v2_halos[1])
-
     kind = 1 - core
 
     def ascend1(r, carry):
@@ -604,12 +635,21 @@
         v1f[at(r), :] = keep_share * mid + weight * (g1[at(r), :] + scaled * total + earlier)
         return carry
 
-    for (start, size), copy in zip(whole, v1f_shift):
-        blocks(start, size, ascend1, 0)
-
-        @pl.when(core == 0)
-        def _():
-            copy.start()
+    for j in (1, 2, 0, 3):
+        if j == 0:
+            finish_halo(v2_halos[0])
+
+            @pl.when(has_second)
+            def _():
+                finish_halo(v2_halos[1])
+
+        chunk(j, ascend1)
+        if j in early_half:
+            @pl.when(core == 0)
+            def _():
+                v1f_shift[j].start()
+        else:
+            send(v1f_shift[j])
 
     def ascend_last(r, carry):
         scaled, _, weight = coefficients(0, r)
@@ -638,17 +678,21 @@
         v1f_e[at(r), :] = keep_share * mid + early + weight * (scaled * total + v1_ee[at(r), :] + above)
         return carry
 
-    for (start, size), arrived, skipped in zip(whole, v1f_shift, skip_shift):
-        @pl.when(core == 1)
-        def _():
-            arrived.wait_recv()
-
-        @pl.when(has_second)
-        def _():
-            skipped.wait_recv()
-            blocks(start, size, ascend_before, 0)
-
-        blocks(start, size, ascend_first, 0)
+    for j in range(4):
+        if j in early_half:
+            @pl.when(core == 1)
+            def _():
+                v1f_shift[j].wait_recv()
+
+            @pl.when(has_second)
+            def _():
+                skip_shift[early_half.index(j)].wait_recv()
+                chunk(j, ascend_before)
+        else:
+            receive(v1f_shift[j])
+
+    for j in range(4):
+        chunk(j, ascend_first)
     stores = pltpu.make_async_copy(sol.at[:, low:high], out, store_sem)
     stores.start()
 
@@ -704,8 +748,8 @@
             @pl.when(jnp.logical_not(last))
             def _():
                 copy.wait_send()
-    for copy in v1f_shift:
-        @pl.when(core == 0)
+    for j, copy in enumerate(v1f_shift):
+        @pl.when((core == 0) if j in early_half else jnp.logical_not(last))
         def _():
             copy.wait_send()
     for copy in skip_shift:
@@ -752,6 +796,7 @@
         plane(), plane(), plane(2),
         coarse(chips), coarse(chips), coarse(chips // 2), coarse(chips // 2), coarse(1), coarse(1), coarse(1),
         (coarse(chips // 2), coarse(chips)),
+        plane(2),
         pltpu.VMEM((TILE, 128), jnp.float32),
         pltpu.VMEM((devices, TILE, 128), jnp.float32),
         pltpu.VMEM((strips, TILE, 128), jnp.float32),

time: 120 us -> 117 us (0.975)
  Pallas kernels: 115 us -> 112 us
    pallas_call x1, Pallas kernels: 115 us -> 112 us  [fast_body(): pl.pallas_call(functools.partial(cycle_kernel, strips, devices, cells), o...]
where the time goes in v3:
time: 117 us
  Pallas kernels  112 us (96%)
  local copies, waits for them, and re-layouts  4.47 us (4%)
    pallas_call x1, Pallas kernels, fast_body(): pl.pallas_call(functools.partial(cycle_kernel, strips, devices, cells), o...  112 us
    unnamed x1, local copies, waits for them, and re-layouts  3.16 us

profile of v3, /device:TPU:0, one launch (start us, length us, event | category | flops | bytes accessed | tf_op | source)
XLA Modules:
  0.0 117.2 jit_solution(17901286769219795282)
XLA Ops:
  0.6 112.1 %shard_map.50 = (f32[2,256,1024]{2,1,0:T(8,128)}, f32[8,128]{1,0:T(8,128)}) custom-call(f32[2,256,1024]{2,1,0:T(8,128)} %rhs_in.1, f32[2,256,1024]{2,1,0:T(8,128)} %guess_in.1, f32[256,1024]{1,0:T(8,128)} %diff_in.1), custom_call_target="tpu_custom_call" | custom-call | tf_op jit(solution)/shard_map/pallas_call | solution.py:809
  112.8 1.3 %slice_reduce_fusion = f32[6]{0:T(128)} fusion(f32[8,128]{1,0:T(8,128)} %get-tuple-element.5), kind=kLoop, calls=%fused_computation | loop fusion | bytes 48 | tf_op jit(solution)/shard_map/slice | solution.py:822
  114.1 3.2 %copy.6 = f32[2,256,1024]{2,1,0:T(8,128)} copy(f32[2,256,1024]{2,1,0:T(8,128)} %get-tuple-element.8) | data formatting | bytes 4194304

commit v4 on v3

--- a/solution.py
+++ b/solution.py
@@ -129,10 +129,10 @@
 def cycle_kernel(
     strips, devices, cells,
     rhs_in, guess_in, diff_in, out, norms_out,
-    rhs, guess, diff, v0, g1, v1, r1, v1f, sol, guess_e, v0_e, v1_e, v1_ee, v1f_e, sol_e,
+    rhs, guess, diff, v0, g1, v1, r1, v1f, sol, guess_e, v0_e, v1_e, v1f_e, sol_e,
     pair, g2h, v2, c_g2, c_v2, c_g3, c_v3, c_g4, c_v4, c_v4b, finals, weights, tile, gathered, gathered_z,
     load_sem, store_sem, zs_sem, zr_sem, ts_sem, tr_sem, ps_sem, pr_sem, as_sem, ar_sem, al_sem,
-    bs_sem, br_sem, bl_sem, rs_sem, es_sem, er_sem, ns_sem, nr_sem, ms_sem, mr_sem,
+    bs_sem, br_sem, bl_sem, rs_sem, credit, ns_sem, nr_sem, ms_sem, mr_sem,
 ):
     me = lax.axis_index("tm")
     strip = lax.axis_index("space")
@@ -297,7 +297,7 @@
     def _():
         def clear(r, carry):
             zero = jnp.zeros((block[0], width), jnp.float32)
-            for ref in (guess_e, v0_e, v1_e, v1_ee, v1f_e, sol_e):
+            for ref in (guess_e, v0_e, v1_e, v1f_e, sol_e):
                 ref[at(r), :] = zero
             v2[1, at(r), :] = zero
             return carry
@@ -412,7 +412,7 @@
         return carry + squares(one, keep) + squares(two, keep)
 
     total0 = zero_tile
-    for j in (1, 2, 0, 3):
+    for j in range(4):
         receive(v0_shift[j])
         total0 = chunk(j, descend, total0)
         send(v1_shift[j])
@@ -426,69 +426,62 @@
         return carry + squares(resid, keep)
 
     total1 = zero_tile
-    for j in (1, 2, 0, 3):
-        receive(v1_shift[j])
-        total1 = chunk(j, residual1, total1)
-
-    mine = aligned(low - TILE + core * half)
-    theirs = aligned(low - TILE + (1 - core) * half)
-    span = half + 2 * TILE
-    swap = tm_copy(
-        r1.at[pl.ds(theirs, span)], pair.at[pl.ds(theirs, span)], ps_sem, pr_sem, me + 1 - 2 * core
-    )
-    swap.start()
-    swap_in = tm_copy(r1.at[pl.ds(mine, span)], pair.at[pl.ds(mine, span)], ps_sem, pr_sem, me + 1 - 2 * core)
-    swap_in.wait_recv()
-
-    def join(r, carry):
-        g2h[at(r), :] = r1[at(r), :] + pair[at(r), :]
-        return carry
-
-    blocks(mine, span, join, 0, TILE)
     tall_piece = piece + 2 * TILE
     c_low, c_high = EDGE, EDGE + piece
     c_rows = slice(c_low - TILE, c_high + TILE)
-    for i in range(chips):
-        owner = core * chips + i
-        src = g2h.at[pl.ds(aligned(low - TILE + owner * piece), tall_piece)]
-        copy = tm_copy(src, c_g2.at[chip, c_rows], as_sem.at[i], ar_sem.at[chip], owner)
-        local = pltpu.make_async_copy(src, c_g2.at[chip, c_rows], al_sem)
-
-        @pl.when(owner == me)
+    sibling = me + 1 - 2 * core
+
+    def swap_of(k):
+        start = low - TILE + k * piece
+        return tm_copy(
+            r1.at[start:start + tall_piece], pair.at[k // 2], ps_sem.at[k // 2], pr_sem.at[k // 2], sibling
+        )
+
+    def hand_over(k):
+        return tm_copy(g2h.at[k // 2], c_g2.at[chip, c_rows], as_sem.at[k // 2], ar_sem.at[chip], k)
+
+    def join_piece(k):
+        start = low - TILE + k * piece
+
+        def join(r, carry):
+            g2h[k // 2, at(r), :] = r1[at(aligned(r + start)), :] + pair[k // 2, at(r), :]
+            return carry
+
+        swap_of(k).wait_recv()
+        blocks(0, tall_piece, join, 0, TILE)
+        local = pltpu.make_async_copy(g2h.at[k // 2], c_g2.at[chip, c_rows], al_sem)
+
+        @pl.when(me == k)
         def _():
             local.start()
             local.wait()
 
-        @pl.when(owner != me)
-        def _():
-            copy.start()
-
-    giver = me // chips
+        @pl.when(me != k)
+        def _():
+            hand_over(k).start()
+
+    done = 0
+    for j in range(4):
+        receive(v1_shift[j])
+        total1 = chunk(j, residual1, total1)
+        ready = (sum(whole[j]) - tall_piece - low + TILE) // piece + 1
+        for k in range(done, ready):
+            @pl.when(core != k % 2)
+            def _():
+                swap_of(k).start()
+        for k in range(done, ready):
+            @pl.when(core == k % 2)
+            def _():
+                join_piece(k)
+        done = ready
     for c in range(chips):
-        copy = tm_copy(
-            g2h.at[pl.ds(low, tall_piece)], c_g2.at[c, c_rows], as_sem.at[0], ar_sem.at[c],
-            lax.rem(me + 1, devices),
-        )
-
-        @pl.when(2 * c + giver != me)
+        copy = tm_copy(g2h.at[0], c_g2.at[c, c_rows], as_sem.at[0], ar_sem.at[c], sibling)
+
+        @pl.when(c != chip)
         def _():
             copy.wait_recv()
 
-    early_half = ()
-    skip_shift = [
-        tm_copy(
-            v1.at[start:start + size], v1_ee.at[start:start + size], es_sem.at[j], er_sem.at[j],
-            jnp.minimum(me + 2, devices - 1),
-        )
-        for j, (start, size) in enumerate(whole) if j in early_half
-    ]
-    sends_skip = jnp.logical_and(core == 0, chip < chips - 1)
     has_second = jnp.logical_and(core == 0, jnp.logical_not(first))
-
-    @pl.when(sends_skip)
-    def _():
-        for copy in skip_shift:
-            copy.start()
 
     offset = me * piece
 
@@ -589,7 +582,6 @@
             def _():
                 copy.start()
 
-    sibling = me + 1 - 2 * core
     relays = []
     for i in range(chips):
         for side in (core, 1 - core):
@@ -626,6 +618,12 @@
     def _():
         start_halo(v2_halos[1])
 
+    sends_on = jnp.logical_and(core == 1, jnp.logical_not(last))
+
+    @pl.when(has_second)
+    def _():
+        pl.semaphore_signal(credit, inc=1, device_id={"tm": me - 1, "space": strip}, device_id_type=DEVICE)
+
     kind = 1 - core
 
     def ascend1(r, carry):
@@ -644,12 +642,11 @@
                 finish_halo(v2_halos[1])
 
         chunk(j, ascend1)
-        if j in early_half:
-            @pl.when(core == 0)
+        if j == 1:
+            @pl.when(sends_on)
             def _():
-                v1f_shift[j].start()
-        else:
-            send(v1f_shift[j])
+                pl.semaphore_wait(credit, 1)
+        send(v1f_shift[j])
 
     def ascend_last(r, carry):
         scaled, _, weight = coefficients(0, r)
@@ -659,9 +656,8 @@
         return carry
 
     blocks(low - TILE, TILE, ascend_last, 0)
-    for (start, size), copy in zip(inner, sol_shift):
+    for start, size in inner:
         blocks(start, size, ascend_last, 0)
-        send(copy)
     blocks(high, TILE, ascend_last, 0)
 
     def ascend_first(r, carry):
@@ -671,27 +667,14 @@
         sol[0, at(r), :] = keep_share * mid + weight * (rhs[0, at(r), :] + scaled * total + earlier)
         return carry
 
-    def ascend_before(r, carry):
-        scaled, _, weight = coefficients(1, r)
-        early, above = v1_e[at(r), :], v2[1, at(r), :]
-        mid, total = stencil(v1_e[tall_at(r), :] + v2[1, tall_at(r), :])
-        v1f_e[at(r), :] = keep_share * mid + early + weight * (scaled * total + v1_ee[at(r), :] + above)
-        return carry
-
     for j in range(4):
-        if j in early_half:
-            @pl.when(core == 1)
-            def _():
-                v1f_shift[j].wait_recv()
-
-            @pl.when(has_second)
-            def _():
-                skip_shift[early_half.index(j)].wait_recv()
-                chunk(j, ascend_before)
-        else:
-            receive(v1f_shift[j])
-
-    for j in range(4):
+        receive(v1f_shift[j])
+
+        @pl.when(jnp.logical_not(last))
+        def _():
+            v1f_shift[j].wait_send()
+            sol_shift[j].start()
+
         chunk(j, ascend_first)
     stores = pltpu.make_async_copy(sol.at[:, low:high], out, store_sem)
     stores.start()
@@ -748,27 +731,16 @@
             @pl.when(jnp.logical_not(last))
             def _():
                 copy.wait_send()
-    for j, copy in enumerate(v1f_shift):
-        @pl.when((core == 0) if j in early_half else jnp.logical_not(last))
-        def _():
-            copy.wait_send()
-    for copy in skip_shift:
-        @pl.when(sends_skip)
-        def _():
-            copy.wait_send()
     for _, copy in relays[0::2]:
         copy.wait_send()
-    swap.wait_send()
-    for i in range(chips):
-        owner = core * chips + i
-        copy = tm_copy(
-            g2h.at[pl.ds(aligned(low - TILE + owner * piece), tall_piece)], c_g2.at[chip, c_rows],
-            as_sem.at[i], ar_sem.at[chip], owner,
-        )
-
-        @pl.when(owner != me)
-        def _():
-            copy.wait_send()
+    for k in range(devices):
+        @pl.when(core != k % 2)
+        def _():
+            swap_of(k).wait_send()
+
+        @pl.when(jnp.logical_and(core == k % 2, me != k))
+        def _():
+            hand_over(k).wait_send()
     for target, copy in back:
         @pl.when(me != target)
         def _():
@@ -789,20 +761,21 @@
     def coarse(count):
         return pltpu.VMEM((count, c_height, width), jnp.float32)
 
+    shared = pltpu.VMEM((chips, rows // devices + EDGE, width), jnp.float32)
     dma = pltpu.SemaphoreType.DMA
     scratch = [
         plane(2), plane(2), plane(), plane(2), plane(), plane(), plane(), plane(), plane(2),
-        plane(), plane(), plane(), plane(), plane(), plane(),
-        plane(), plane(), plane(2),
+        plane(), plane(), plane(), plane(), plane(),
+        shared, shared, plane(2),
         coarse(chips), coarse(chips), coarse(chips // 2), coarse(chips // 2), coarse(1), coarse(1), coarse(1),
         (coarse(chips // 2), coarse(chips)),
         plane(2),
         pltpu.VMEM((TILE, 128), jnp.float32),
         pltpu.VMEM((devices, TILE, 128), jnp.float32),
         pltpu.VMEM((strips, TILE, 128), jnp.float32),
-        dma((3,)), dma, dma((5, 2)), dma((5, 2)), dma((5, 4)), dma((5, 4)), dma, dma,
+        dma((3,)), dma, dma((5, 2)), dma((5, 2)), dma((5, 4)), dma((5, 4)), dma((chips,)), dma((chips,)),
         dma((chips,)), dma((chips,)), dma, dma((2, devices)), dma((2, devices)), dma((2,)),
-        dma((chips,)), dma((4,)), dma((4,)),
+        dma((chips,)), pltpu.SemaphoreType.REGULAR,
         dma((devices,)), dma((devices,)), dma((strips,)), dma((strips,)),
     ]
     any_space = pl.BlockSpec(memory_space=pl.ANY)

time: 117 us -> 110 us (0.940)
  Pallas kernels: 112 us -> 105 us
    pallas_call x1, Pallas kernels: 112 us -> 105 us  [fast_body(): pl.pallas_call(functools.partial(cycle_kernel, strips, devices, cells), o...]
where the time goes in v4:
time: 110 us
  Pallas kernels  105 us (95%)
  local copies, waits for them, and re-layouts  4.47 us (4%)
    pallas_call x1, Pallas kernels, fast_body(): pl.pallas_call(functools.partial(cycle_kernel, strips, devices, cells), o...  105 us
    unnamed x1, local copies, waits for them, and re-layouts  3.16 us

profile of v4, /device:TPU:0, one launch (start us, length us, event | category | flops | bytes accessed | tf_op | source)
XLA Modules:
  0.0 110.3 jit_solution(12264002852239345384)
XLA Ops:
  0.6 105.2 %shard_map.50 = (f32[2,256,1024]{2,1,0:T(8,128)}, f32[8,128]{1,0:T(8,128)}) custom-call(f32[2,256,1024]{2,1,0:T(8,128)} %rhs_in.1, f32[2,256,1024]{2,1,0:T(8,128)} %guess_in.1, f32[256,1024]{1,0:T(8,128)} %diff_in.1), custom_call_target="tpu_custom_call" | custom-call | tf_op jit(solution)/shard_map/pallas_call | solution.py:782
  105.8 1.3 %slice_reduce_fusion = f32[6]{0:T(128)} fusion(f32[8,128]{1,0:T(8,128)} %get-tuple-element.5), kind=kLoop, calls=%fused_computation | loop fusion | bytes 48 | tf_op jit(solution)/shard_map/slice | solution.py:795
  107.2 3.2 %copy.6 = f32[2,256,1024]{2,1,0:T(8,128)} copy(f32[2,256,1024]{2,1,0:T(8,128)} %get-tuple-element.8) | data formatting | bytes 4194304

commit v5 on v4

--- a/solution.py
+++ b/solution.py
@@ -782,14 +782,14 @@
     result, norms = pl.pallas_call(
         functools.partial(cycle_kernel, strips, devices, cells),
         out_shape=(
-            jax.ShapeDtypeStruct(rhs.shape, jnp.float32),
+            pltpu.VMEM(rhs.shape, jnp.float32),
             jax.ShapeDtypeStruct((TILE, 128), jnp.float32),
         ),
         in_specs=[any_space] * 3,
-        out_specs=(any_space, pl.BlockSpec(memory_space=pltpu.VMEM)),
+        out_specs=(pl.BlockSpec(memory_space=pltpu.VMEM), pl.BlockSpec(memory_space=pltpu.VMEM)),
         scratch_shapes=scratch,
         compiler_params=pltpu.CompilerParams(
-            collective_id=0, has_side_effects=True, vmem_limit_bytes=60 * 2**20
+            collective_id=0, has_side_effects=True, vmem_limit_bytes=67_043_328 - rhs.size * 4 - 2**17
         ),
     )(rhs, guess, diffusion)
     return result, norms[:LEVELS + 1, 0]

time: 110 us -> 108 us (0.982)
  local copies, waits for them, and re-layouts: 4.47 us -> 1.95 us
    unnamed x1 -> x3, local copies, waits for them, and re-layouts: 3.16 us -> 1.33 us
where the time goes in v5:
time: 108 us
  Pallas kernels  105 us (97%)
  local copies, waits for them, and re-layouts  1.95 us (2%)
    pallas_call x1, Pallas kernels, fast_body(): pl.pallas_call(functools.partial(cycle_kernel, strips, devices, cells), o...  105 us

profile of v5, /device:TPU:0, one launch (start us, length us, event | category | flops | bytes accessed | tf_op | source)
XLA Modules:
  0.0 107.8 jit_solution(4943541214677913914)
XLA Ops:
  0.6 105.2 %shard_map.50 = (f32[2,256,1024]{2,1,0:T(8,128)S(1)}, f32[8,128]{1,0:T(8,128)}) custom-call(f32[2,256,1024]{2,1,0:T(8,128)} %rhs_in.1, f32[2,256,1024]{2,1,0:T(8,128)} %guess_in.1, f32[256,1024]{1,0:T(8,128)} %diff_in.1), custom_call_target="tpu_custom_call" | custom-call | tf_op jit(solution)/shard_map/pallas_call | solution.py:782
  105.8 0.0 copy-start
  105.8 1.3 %copy.6 = f32[2,256,1024]{2,1,0:T(8,128)} copy(f32[2,256,1024]{2,1,0:T(8,128)S(1)} %get-tuple-element.6) | data formatting | bytes 4194304
  107.2 0.0 copy-done
  107.2 0.6 slice_reduce_fusion
Async XLA Ops:
  105.8 1.3 %copy-start = (f32[8,128]{1,0:T(8,128)S(1)}, f32[8,128]{1,0:T(8,128)}, u32[]{:S(2)}) copy-start(f32[8,128]{1,0:T(8,128)} %get-tuple-element.5) | copy-start | bytes 12292
